TPU v7x, 256 devices: a whole 4x4x8 slice. The times are simulated.
256 devices in a mesh: row: 8 (over x, core), col: 32 (over y, z).
Axes of the slice: x: 4, y: 4, z: 8, core: 2. Of those that a mesh axis runs over, the one named last changes fastest.
Arguments:
- rhs: float32 [8, 32, 8, 4, 128], P('row', 'col'), may hold values from -6 to 6
- diag0: float32 [8, 32, 8, 128], P('row', 'col'), may hold values from 2 to 4
- blocks0: float32 [8, 32, 8, 14, 128, 128], P('row', 'col'), may hold values from -0.1875 to 0.1875
- cols0: int32 [8, 32, 8, 14], P('row', 'col'), may hold values from 0 to 23
- sends0: int32 [8, 32, 4, 4], P('row', 'col'), may hold values from 0 to 7
- pro0: float32 [8, 32, 8, 128, 128], P('row', 'col'), may hold values from -0.5 to 0.5
- agg0: int32 [8, 32, 8], P('row', 'col'), may hold values from 0 to 1
- diag1: float32 [8, 32, 2, 128], P('row', 'col'), may hold values from 2 to 4
- blocks1: float32 [8, 32, 2, 14, 128, 128], P('row', 'col'), may hold values from -0.1875 to 0.1875
- cols1: int32 [8, 32, 2, 14], P('row', 'col'), may hold values from 0 to 9
- sends1: int32 [8, 32, 4, 2], P('row', 'col'), may hold values from 0 to 1
- pro1: float32 [8, 32, 2, 128, 128], P('row', 'col'), may hold values from -0.25 to 0.25
- agg1: int32 [8, 32, 2], P('row', 'col'), may hold values from 0 to 63
- cinv: float32 [8192, 8192], P(('row', 'col')), may hold values from -0.0625 to 0.0625
Outputs:
- solution: float32 [8, 32, 8, 4, 128], P('row', 'col')
Inputs may be any that keep to these rules, and one draw needn't show every extreme that they name: `sends0`: indices of the sender's own fine blocks. `sends1`: indices of the sender's own level-one blocks. `cols0`: indices into the extended fine vector of 24 blocks. `cols1`: indices into the extended level-one vector of 10 blocks. `agg0`: a level-one block of the same partition. `agg1`: a coarsest block, on any partition.
All inputs are finite; a program needn't handle non-finite values.
Results may differ from a plain program's by a relative error of at most 0.0001.
Values sent between devices are 32-bit elements; how exact they have to be, the bound alone decides.
A program may use at most 64 MiB of HBM per device.

v0:
```python
import functools

import jax
import jax.numpy as jnp
from jax import lax
from jax.sharding import Mesh
from jax.sharding import PartitionSpec as P

NU = 2
ROW_COL = ("row_0", "row_1", "col_0", "col_1")
ROW = ("row_0", "row_1")
COL = ("col_0", "col_1")


HIGH = lax.Precision.HIGHEST
OMEGA = 0.3


def extended_2(value, sides, width):
    edges = {}
    for axis, dim in sides:
        size, length = (lax.axis_size(axis), value.shape[dim])
        up = [(i, (i + 1) % size) for i in range(size - 1)]
        last = lax.slice_in_dim(value, length - width, length, axis=dim)
        leading = lax.slice_in_dim(value, 0, width, axis=dim)
        edges[dim] = (
            lax.ppermute(last, axis, up),
            lax.ppermute(leading, axis, [(b, a) for a, b in up]),
        )
    done = []
    for _, dim in sides:
        low, high = edges[dim]
        around = [(width, width) if d in done else (0, 0) for d in range(value.ndim)]
        value = jnp.concatenate([jnp.pad(low, around), value, jnp.pad(high, around)], axis=dim)
        done.append(dim)
    return value


def by_axis(value, axes):
    return functools.reduce(lax.psum, axes, value)


def gather_ghosts(vector, sends):
    packed = vector[sends]
    padded = extended_2(packed[None, None], ((ROW, 0), (COL, 1)), 1)
    return jnp.concatenate(
        [vector, padded[0, 1, 0], padded[2, 1, 1], padded[1, 0, 2], padded[1, 2, 3]], axis=0
    )


def apply_op(vector, diag, blocks, cols, sends):
    extended = gather_ghosts(vector, sends)
    nearby = extended[cols]
    coupled = jnp.einsum("bkij,bkrj->bri", blocks, nearby, precision=HIGH)
    return diag[:, None, :] * vector + coupled


def smooth(vector, right_side, diag, blocks, cols, sends, count):
    for sweep in range(count):
        vector = (
            vector
            + OMEGA * (right_side - apply_op(vector, diag, blocks, cols, sends)) / diag[:, None, :]
        )
    return vector


def on_device(
    rhs, diag0, blocks0, cols0, sends0, pro0, agg0, diag1, blocks1, cols1, sends1, pro1, agg1, cinv
):
    fine_rhs = rhs[0, 0]
    fine_diag = diag0[0, 0]
    fine_blocks = blocks0[0, 0]
    fine_cols = cols0[0, 0]
    fine_sends = sends0[0, 0]
    fine_pro = pro0[0, 0]
    level_diag = diag1[0, 0]
    level_blocks = blocks1[0, 0]
    level_cols = cols1[0, 0]
    level_sends = sends1[0, 0]
    level_pro = pro1[0, 0]
    level_count = level_diag.shape[0]
    block_size = level_diag.shape[1]
    loads = fine_rhs.shape[1]
    coarse_total = cinv.shape[1]
    coarse_count = coarse_total // block_size
    fine_x = OMEGA * fine_rhs / fine_diag[:, None, :]
    fine_x = smooth(fine_x, fine_rhs, fine_diag, fine_blocks, fine_cols, fine_sends, NU - 1)
    fine_res = fine_rhs - apply_op(fine_x, fine_diag, fine_blocks, fine_cols, fine_sends)
    onehot0 = (agg0[0, 0][:, None] == jnp.arange(level_count)).astype(jnp.float32)
    restricted = jnp.einsum("bij,bri->brj", fine_pro, fine_res, precision=HIGH)
    level_rhs = jnp.einsum("bc,brj->crj", onehot0, restricted, precision=HIGH)
    level_x = OMEGA * level_rhs / level_diag[:, None, :]
    level_x = smooth(level_x, level_rhs, level_diag, level_blocks, level_cols, level_sends, NU - 1)
    level_res = level_rhs - apply_op(level_x, level_diag, level_blocks, level_cols, level_sends)
    onehot1 = (agg1[0, 0][:, None] == jnp.arange(coarse_count)).astype(jnp.float32)
    contrib = jnp.einsum("bij,bri->brj", level_pro, level_res, precision=HIGH)
    term = jnp.einsum("bc,brj->rcj", onehot1, contrib, precision=HIGH).reshape(loads, coarse_total)
    coarse_rhs = by_axis(term, ROW_COL)
    own_rows = jnp.einsum("ij,rj->ri", cinv, coarse_rhs, precision=HIGH)
    coarse_x = lax.all_gather(own_rows, ROW_COL, axis=1, tiled=True)
    coarse_blocks = coarse_x.reshape(loads, coarse_count, block_size)
    picked = jnp.einsum("bc,rcj->brj", onehot1, coarse_blocks, precision=HIGH)
    level_x = level_x + jnp.einsum("bij,brj->bri", level_pro, picked, precision=HIGH)
    level_x = smooth(level_x, level_rhs, level_diag, level_blocks, level_cols, level_sends, NU)
    lifted = jnp.einsum("bc,crj->brj", onehot0, level_x, precision=HIGH)
    fine_x = fine_x + jnp.einsum("bij,brj->bri", fine_pro, lifted, precision=HIGH)
    fine_x = smooth(fine_x, fine_rhs, fine_diag, fine_blocks, fine_cols, fine_sends, NU)
    return fine_x[None, None]


def solution(mesh):
    finer = Mesh(mesh.devices.reshape(4, 2, 4, 8), ("row_0", "row_1", "col_0", "col_1"))
    in_specs = (
        P(ROW, COL, None, None, None),
        P(ROW, COL, None, None),
        P(ROW, COL, None, None, None, None),
        P(ROW, COL, None, None),
        P(ROW, COL, None, None),
        P(ROW, COL, None, None, None),
        P(ROW, COL, None),
        P(ROW, COL, None, None),
        P(ROW, COL, None, None, None, None),
        P(ROW, COL, None, None),
        P(ROW, COL, None, None),
        P(ROW, COL, None, None, None),
        P(ROW, COL, None),
        P(ROW_COL, None),
    )
    out_specs = P(ROW, COL, None, None, None)
    return jax.shard_map(
        on_device, mesh=finer, in_specs=in_specs, out_specs=out_specs, check_vma=False
    )
```

profile of v0, /device:TPU:8, one launch (start us, length us, event | category | flops | bytes accessed | tf_op | source)
XLA Modules:
  0.0 488.9 jit_solution(9224719478229903555)
XLA Ops:
  10.3 7.6 %collective-permute-start.3 = (f32[1,1,4,4,4,128]{5,4,3,2,1,0:T(4,128)S(1)}, f32[1,1,4,4,4,128]{5,4,3,2,1,0:T(4,128)S(1)}, u32[]{:S(2)}, u32[]{:S(2)}) collective-permute-start(f32[1,1,4,4,4,128]{5,4,3,2,1,0:T(4,128)S(1)} %bitcast.456), channel_id=1, source_target_pairs={{1,0},{2,1},{3,2},{4,3},{5,4},{6,5},{7,6},{8,7},{9,8},{10,9},{11,1... | collective-permute-start | bytes 98312 | tf_op jit(solution)/shard_map/ppermute | solution.py:28
  17.9 1.9 collective-permute-start.2
  19.8 1.3 collective-permute-start.1
  21.1 3.0 collective-permute-start
  26.6 8.3 %constant_dynamic-update-slice_fusion.9 = (f32[24,4,128]{2,1,0:T(4,128)S(1)}, f32[8,4,128]{2,1,0:T(4,128)S(1)}) fusion(f32[8,14,4,128]{3,2,1,0:T(4,128)S(1)} %bitcast.438, f32[1,1,8,14,128,128]{5,4,3,2,1,0:T(8,128)} %param.16, f32[8,128]{1,0:T(8,128)} %bitcast.448, f32[1,1,8,4,128]{4,3,2,1,0:T(4,128)} %param.14), kind=kOutput, calls=%fused_computation.98 | convolution fusion | flops 88113152 | bytes 7622656 | tf_op jit(solution)/shard_map/bkij,bkrj->bri/dot_general | solution.py:54
  35.5 3.0 collective-permute-start.4
  39.2 6.0 %collective-permute-start.7 = (f32[1,1,4,4,4,128]{5,4,3,2,1,0:T(4,128)S(1)}, f32[1,1,4,4,4,128]{5,4,3,2,1,0:T(4,128)S(1)}, u32[]{:S(2)}, u32[]{:S(2)}) collective-permute-start(f32[1,1,4,4,4,128]{5,4,3,2,1,0:T(4,128)S(1)} %bitcast.461), channel_id=1, source_target_pairs={{1,0},{2,1},{3,2},{4,3},{5,4},{6,5},{7,6},{8,7},{9,8},{10,9},{11,1... | collective-permute-start | bytes 98312 | tf_op jit(solution)/shard_map/ppermute | solution.py:28
  45.2 1.9 collective-permute-start.6
  47.1 1.3 collective-permute-start.5
  49.2 2.0 collective-permute-done.5
  51.2 1.9 collective-permute-done.6
  53.2 1.4 gather_fusion.3
  54.6 9.2 %fusion.64 = f32[8,4,128]{2,1,0:T(4,128)S(1)} fusion(f32[8,14,4,128]{3,2,1,0:T(4,128)} %bitcast.440, f32[1,1,8,14,128,128]{5,4,3,2,1,0:T(8,128)} %param.16, f32[1,1,8,4,128]{4,3,2,1,0:T(4,128)S(1)} %copy-done.4, f32[8,4,128]{2,1,0:T(4,128)} %copy-done.5, f32[8,128]{1,0:T(8,128)} %bitcast.449), kind=kOutput, calls=%fused_computation.50 | convolution fusion | flops 88092672 | bytes 7622656 | tf_op jit(solution)/shard_map/bkij,bkrj->bri/dot_general | solution.py:54
  65.7 1.3 multiply_divide_fusion
  67.0 2.0 gather_fusion.4
  69.7 2.6 collective-permute-start.8
  73.6 5.7 %collective-permute-start.11 = (f32[1,1,4,2,4,128]{5,4,3,2,1,0:T(4,128)S(1)}, f32[1,1,4,2,4,128]{5,4,3,2,1,0:T(4,128)S(1)}, u32[]{:S(2)}, u32[]{:S(2)}) collective-permute-start(f32[1,1,4,2,4,128]{5,4,3,2,1,0:T(4,128)S(1)} %copy.98), channel_id=1, source_target_pairs={{1,0},{2,1},{3,2},{4,3},{5,4},{6,5},{7,6},{8,7},{9,8},{10,9},{11,1... | collective-permute-start | bytes 49160 | tf_op jit(solution)/shard_map/ppermute | solution.py:28
  79.3 1.9 collective-permute-start.10
  81.3 1.3 collective-permute-start.9
  84.9 2.1 collective-permute-done.10
  88.3 2.1 gather_fusion.5
  90.3 3.1 constant_dynamic-update-slice_fusion.19
  93.4 2.0 gather_fusion.6
  96.1 1.9 collective-permute-start.12
  98.0 5.7 %collective-permute-start.15 = (f32[1,1,4,2,4,128]{5,4,3,2,1,0:T(4,128)S(1)}, f32[1,1,4,2,4,128]{5,4,3,2,1,0:T(4,128)S(1)}, u32[]{:S(2)}, u32[]{:S(2)}) collective-permute-start(f32[1,1,4,2,4,128]{5,4,3,2,1,0:T(4,128)S(1)} %copy.104), channel_id=1, source_target_pairs={{1,0},{2,1},{3,2},{4,3},{5,4},{6,5},{7,6},{8,7},{9,8},{10,9},{11,1... | collective-permute-start | bytes 49160 | tf_op jit(solution)/shard_map/ppermute | solution.py:28
  103.7 1.9 collective-permute-start.14
  105.7 1.5 collective-permute-start.13
  109.3 2.1 collective-permute-done.14
  112.7 2.1 gather_fusion.7
  114.7 2.4 fusion.127
  119.2 44.8 %all-reduce.5.cloned.1.call-done = f32[4,8192]{1,0:T(4,128)} async-done(((f32[4,8192]{1,0:T(4,128)}), f32[4,8192]{1,0:T(4,128)}) %all-reduce.5.cloned.1.call-update) | async-done | bytes 131088 | tf_op jit(solution)/shard_map/psum | solution.py:40
  164.1 31.7 %all-reduce.7.cloned.1.call-done = f32[4,8192]{1,0:T(4,128)} async-done(((f32[4,8192]{1,0:T(4,128)}), f32[4,8192]{1,0:T(4,128)}) %all-reduce.7.cloned.1.call-update) | async-done | bytes 131088 | tf_op jit(solution)/shard_map/psum | solution.py:40
  195.9 49.0 %all-reduce.9.cloned.1.call-done = f32[4,8192]{1,0:T(4,128)} async-done(((f32[4,8192]{1,0:T(4,128)}), f32[4,8192]{1,0:T(4,128)}) %all-reduce.9.cloned.1.call-update) | async-done | bytes 131088 | tf_op jit(solution)/shard_map/psum | solution.py:40
  244.8 76.3 %all-reduce.11.cloned.1.call-done = f32[4,8192]{1,0:T(4,128)} async-done(((f32[4,8192]{1,0:T(4,128)}), f32[4,8192]{1,0:T(4,128)}) %all-reduce.11.cloned.1.call-update) | async-done | bytes 131088 | tf_op jit(solution)/shard_map/psum | solution.py:40
  321.2 1.8 convolution_bitcast_fusion.1
  323.0 70.0 %all-gather = f32[256,32,4]{1,2,0:T(4,128)S(1)} all-gather(f32[1,32,4]{1,2,0:T(4,128)S(1)} %convolution_bitcast_fusion.1), channel_id=1, replica_groups=mesh['row_0'=4,'row_1'=2,'col_0'=4,'col_1'=8] {'row_0','row_1','col_0','..., dimensions={0}, use_global_device_ids=true | all-gather | bytes 131584 | tf_op jit(solution)/shard_map/all_gather | solution.py:100
  395.9 1.3 collective-permute-start.16
  397.1 4.6 collective-permute-start.19
  401.8 1.9 collective-permute-start.18
  403.7 1.3 collective-permute-start.17
  405.0 1.8 collective-permute-done.17
  406.8 2.7 collective-permute-done.18
  410.2 2.3 constant_dynamic-update-slice_fusion.29
  413.3 1.3 collective-permute-start.20
  414.6 4.9 %collective-permute-start.23 = (f32[1,1,4,2,4,128]{5,4,3,2,1,0:T(4,128)S(1)}, f32[1,1,4,2,4,128]{5,4,3,2,1,0:T(4,128)S(1)}, u32[]{:S(2)}, u32[]{:S(2)}) collective-permute-start(f32[1,1,4,2,4,128]{5,4,3,2,1,0:T(4,128)S(1)} %copy.119), channel_id=1, source_target_pairs={{1,0},{2,1},{3,2},{4,3},{5,4},{6,5},{7,6},{8,7},{9,8},{10,9},{11,1... | collective-permute-start | bytes 49160 | tf_op jit(solution)/shard_map/ppermute | solution.py:28
  419.5 1.9 collective-permute-start.22
  421.4 1.3 collective-permute-start.21
  422.8 1.8 collective-permute-done.21
  424.5 2.7 collective-permute-done.22
  428.0 2.3 fusion.106
  431.2 1.6 constant_dynamic-update-slice_fusion.34
  433.4 1.3 collective-permute-start.24
  434.7 5.7 %collective-permute-start.27 = (f32[1,1,4,4,4,128]{5,4,3,2,1,0:T(4,128)S(1)}, f32[1,1,4,4,4,128]{5,4,3,2,1,0:T(4,128)S(1)}, u32[]{:S(2)}, u32[]{:S(2)}) collective-permute-start(f32[1,1,4,4,4,128]{5,4,3,2,1,0:T(4,128)S(1)} %bitcast.469), channel_id=1, source_target_pairs={{1,0},{2,1},{3,2},{4,3},{5,4},{6,5},{7,6},{8,7},{9,8},{10,9},{11,1... | collective-permute-start | bytes 98312 | tf_op jit(solution)/shard_map/ppermute | solution.py:28
  440.5 1.9 collective-permute-start.26
  442.4 1.3 collective-permute-start.25
  443.7 1.8 collective-permute-done.25
  445.5 2.9 collective-permute-done.26
  449.1 8.2 %constant_dynamic-update-slice_fusion.39 = (f32[24,4,128]{2,1,0:T(4,128)S(1)}, f32[8,4,128]{2,1,0:T(4,128)S(1)}) fusion(f32[8,4,128]{2,1,0:T(4,128)S(1)} %get-tuple-element.18, f32[8,14,4,128]{3,2,1,0:T(4,128)S(1)} %bitcast.437, f32[1,1,8,14,128,128]{5,4,3,2,1,0:T(8,128)} %param.16, f32[8,128]{1,0:T(8,128)S(1)} %bitcast.450, ...), kind=kOutput, calls=%fused_computation.128 | convolution fusion | flops 88104960 | bytes 7639040 | tf_op jit(solution)/shard_map/bkij,bkrj->bri/dot_general | solution.py:54
  459.3 5.6 %collective-permute-start.31 = (f32[1,1,4,4,4,128]{5,4,3,2,1,0:T(4,128)S(1)}, f32[1,1,4,4,4,128]{5,4,3,2,1,0:T(4,128)S(1)}, u32[]{:S(2)}, u32[]{:S(2)}) collective-permute-start(f32[1,1,4,4,4,128]{5,4,3,2,1,0:T(4,128)S(1)} %bitcast.465), channel_id=1, source_target_pairs={{1,0},{2,1},{3,2},{4,3},{5,4},{6,5},{7,6},{8,7},{9,8},{10,9},{11,1... | collective-permute-start | bytes 98312 | tf_op jit(solution)/shard_map/ppermute | solution.py:28
  464.9 1.9 collective-permute-start.30
  466.8 1.5 collective-permute-start.29
  468.3 1.6 collective-permute-done.29
  469.9 2.9 collective-permute-done.30
  473.5 8.8 %fusion.43 = f32[1,1,8,4,128]{4,3,2,1,0:T(4,128)} fusion(f32[8,4,128]{2,1,0:T(4,128)S(1)} %get-tuple-element.20, f32[8,14,4,128]{3,2,1,0:T(4,128)S(1)} %bitcast.439, f32[1,1,8,14,128,128]{5,4,3,2,1,0:T(8,128)} %param.16, f32[1,1,8,4,128]{4,3,2,1,0:T(4,128)S(1)} %copy-done.4, f32[8,128]{1,0:T(8,128)S(1)} %bitcast.451), kind=kOutput, calls=%fused_computation.43 | convolution fusion | flops 88104960 | bytes 7622656 | tf_op jit(solution)/shard_map/bkij,bkrj->bri/dot_general | solution.py:54
  (129 shorter events, 31.8 us)
Async XLA Ops:
  6.5 83.8 %copy-start = (f32[1,1,2,14,128,128]{5,4,3,2,1,0:T(8,128)S(1)}, f32[1,1,2,14,128,128]{5,4,3,2,1,0:T(8,128)}, u32[]{:S(2)}) copy-start(f32[1,1,2,14,128,128]{5,4,3,2,1,0:T(8,128)} %param.22) | copy-start | bytes 5505028
  6.5 48.1 %copy-start.4 = (f32[1,1,8,4,128]{4,3,2,1,0:T(4,128)S(1)}, f32[1,1,8,4,128]{4,3,2,1,0:T(4,128)}, u32[]{:S(2)}) copy-start(f32[1,1,8,4,128]{4,3,2,1,0:T(4,128)} %param.14) | copy-start | bytes 49156
  6.5 32.0 %copy-start.12 = (s32[1,1,2,14]{3,2,1,0:T(2,128)S(1)}, s32[1,1,2,14]{3,2,1,0:T(2,128)}, u32[]{:S(2)}) copy-start(s32[1,1,2,14]{3,2,1,0:T(2,128)} %param.23) | copy-start | bytes 340
  6.5 157.4 %all-reduce.5.cloned.1.call-start = ((), (), s32[]{:S(2)}) async-start(), calls=%async_computation | async-start | bytes 262144 | tf_op jit(solution)/shard_map/psum | solution.py:40
  8.9 44.2 %copy-start.10 = (s32[1024]{0:T(1024)}, s32[1024]{0:T(1024)S(1)}, u32[]{:S(2)}) copy-start(s32[1024]{0:T(1024)S(1)} %get-tuple-element.22) | copy-start | bytes 12292
  10.3 15.6 %collective-permute-start.3 = (f32[1,1,4,4,4,128]{5,4,3,2,1,0:T(4,128)S(1)}, f32[1,1,4,4,4,128]{5,4,3,2,1,0:T(4,128)S(1)}, u32[]{:S(2)}, u32[]{:S(2)}) collective-permute-start(f32[1,1,4,4,4,128]{5,4,3,2,1,0:T(4,128)S(1)} %bitcast.456), channel_id=1, source_target_pairs={{1,0},{2,1},{3,2},{4,3},{5,4},{6,5},{7,6},{8,7},{9,8},{10,9},{11,1... | collective-permute-start | bytes 98312 | tf_op jit(solution)/shard_map/ppermute | solution.py:28
  17.9 7.9 %collective-permute-start.2 = (f32[1,1,4,4,4,128]{5,4,3,2,1,0:T(4,128)S(1)}, f32[1,1,4,4,4,128]{5,4,3,2,1,0:T(4,128)S(1)}, u32[]{:S(2)}, u32[]{:S(2)}) collective-permute-start(f32[1,1,4,4,4,128]{5,4,3,2,1,0:T(4,128)S(1)} %bitcast.457), channel_id=1, source_target_pairs={{0,1},{1,2},{2,3},{3,4},{4,5},{5,6},{6,7},{7,8},{8,9},{9,10},{10,1... | collective-permute-start | bytes 98312 | tf_op jit(solution)/shard_map/ppermute | solution.py:27
  19.8 5.2 %collective-permute-start.1 = (f32[1,1,4,4,4,128]{5,4,3,2,1,0:T(4,128)S(1)}, f32[1,1,4,4,4,128]{5,4,3,2,1,0:T(4,128)S(1)}, u32[]{:S(2)}, u32[]{:S(2)}) collective-permute-start(f32[1,1,4,4,4,128]{5,4,3,2,1,0:T(4,128)S(1)} %bitcast.458), channel_id=1, source_target_pairs={{32,0},{64,32},{96,64},{128,96},{160,128},{192,160},{224,192},{33,... | collective-permute-start | bytes 98312 | tf_op jit(solution)/shard_map/ppermute | solution.py:28
  21.1 3.9 collective-permute-start
  25.0 28.2 %copy-start.8 = (s32[1024]{0:T(1024)}, s32[1024]{0:T(1024)S(1)}, u32[]{:S(2)}) copy-start(s32[1024]{0:T(1024)S(1)} %pad_clamp_fusion.2) | copy-start | bytes 12292
  26.6 37.2 %copy-start.1 = (f32[1,1,8,128,128]{4,3,2,1,0:T(8,128)S(1)}, f32[1,1,8,128,128]{4,3,2,1,0:T(8,128)}, u32[]{:S(2)}) copy-start(f32[1,1,8,128,128]{4,3,2,1,0:T(8,128)} %param.19) | copy-start | bytes 1572868
  34.9 18.3 %copy-start.5 = (f32[8,4,128]{2,1,0:T(4,128)}, f32[8,4,128]{2,1,0:T(4,128)S(1)}, u32[]{:S(2)}) copy-start(f32[8,4,128]{2,1,0:T(4,128)S(1)} %get-tuple-element.10) | copy-start | bytes 49156
  34.9 286.2 %copy-start.2 = (f32[32,8192]{1,0:T(8,128)S(1)}, f32[32,8192]{1,0:T(8,128)}, u32[]{:S(2)}) copy-start(f32[32,8192]{1,0:T(8,128)} %param.27) | copy-start | bytes 3145732
  35.5 12.9 %collective-permute-start.4 = (f32[1,1,4,4,4,128]{5,4,3,2,1,0:T(4,128)S(1)}, f32[1,1,4,4,4,128]{5,4,3,2,1,0:T(4,128)}, u32[]{:S(2)}, u32[]{:S(2)}) collective-permute-start(f32[1,1,4,4,4,128]{5,4,3,2,1,0:T(4,128)S(1)} %bitcast.460), channel_id=1, source_target_pairs={{0,32},{32,64},{64,96},{96,128},{128,160},{160,192},{192,224},{1,3... | collective-permute-start | bytes 98312 | tf_op jit(solution)/shard_map/ppermute | solution.py:27
  39.2 14.0 %collective-permute-start.7 = (f32[1,1,4,4,4,128]{5,4,3,2,1,0:T(4,128)S(1)}, f32[1,1,4,4,4,128]{5,4,3,2,1,0:T(4,128)S(1)}, u32[]{:S(2)}, u32[]{:S(2)}) collective-permute-start(f32[1,1,4,4,4,128]{5,4,3,2,1,0:T(4,128)S(1)} %bitcast.461), channel_id=1, source_target_pairs={{1,0},{2,1},{3,2},{4,3},{5,4},{6,5},{7,6},{8,7},{9,8},{10,9},{11,1... | collective-permute-start | bytes 98312 | tf_op jit(solution)/shard_map/ppermute | solution.py:28
  45.2 7.9 %collective-permute-start.6 = (f32[1,1,4,4,4,128]{5,4,3,2,1,0:T(4,128)S(1)}, f32[1,1,4,4,4,128]{5,4,3,2,1,0:T(4,128)S(1)}, u32[]{:S(2)}, u32[]{:S(2)}) collective-permute-start(f32[1,1,4,4,4,128]{5,4,3,2,1,0:T(4,128)S(1)} %bitcast.462), channel_id=1, source_target_pairs={{0,1},{1,2},{2,3},{3,4},{4,5},{5,6},{6,7},{7,8},{8,9},{9,10},{10,1... | collective-permute-start | bytes 98312 | tf_op jit(solution)/shard_map/ppermute | solution.py:27
  47.1 4.1 collective-permute-start.5
  54.6 62.6 %copy-start.3 = (f32[1,1,2,128,128]{4,3,2,1,0:T(8,128)S(1)}, f32[1,1,2,128,128]{4,3,2,1,0:T(8,128)}, u32[]{:S(2)}) copy-start(f32[1,1,2,128,128]{4,3,2,1,0:T(8,128)} %param.25) | copy-start | bytes 393220
  65.1 0.6 copy-start.6
  69.7 12.9 %collective-permute-start.8 = (f32[1,1,4,2,4,128]{5,4,3,2,1,0:T(4,128)S(1)}, f32[1,1,4,2,4,128]{5,4,3,2,1,0:T(4,128)S(1)}, u32[]{:S(2)}, u32[]{:S(2)}) collective-permute-start(f32[1,1,4,2,4,128]{5,4,3,2,1,0:T(4,128)S(1)} %copy.98), channel_id=1, source_target_pairs={{0,32},{32,64},{64,96},{96,128},{128,160},{160,192},{192,224},{1,3... | collective-permute-start | bytes 49160 | tf_op jit(solution)/shard_map/ppermute | solution.py:27
  73.6 14.1 %collective-permute-start.11 = (f32[1,1,4,2,4,128]{5,4,3,2,1,0:T(4,128)S(1)}, f32[1,1,4,2,4,128]{5,4,3,2,1,0:T(4,128)S(1)}, u32[]{:S(2)}, u32[]{:S(2)}) collective-permute-start(f32[1,1,4,2,4,128]{5,4,3,2,1,0:T(4,128)S(1)} %copy.98), channel_id=1, source_target_pairs={{1,0},{2,1},{3,2},{4,3},{5,4},{6,5},{7,6},{8,7},{9,8},{10,9},{11,1... | collective-permute-start | bytes 49160 | tf_op jit(solution)/shard_map/ppermute | solution.py:28
  79.3 7.7 %collective-permute-start.10 = (f32[1,1,4,2,4,128]{5,4,3,2,1,0:T(4,128)S(1)}, f32[1,1,4,2,4,128]{5,4,3,2,1,0:T(4,128)S(1)}, u32[]{:S(2)}, u32[]{:S(2)}) collective-permute-start(f32[1,1,4,2,4,128]{5,4,3,2,1,0:T(4,128)S(1)} %copy.98), channel_id=1, source_target_pairs={{0,1},{1,2},{2,3},{3,4},{4,5},{5,6},{6,7},{7,8},{8,9},{9,10},{10,1... | collective-permute-start | bytes 49160 | tf_op jit(solution)/shard_map/ppermute | solution.py:27
  81.3 3.1 collective-permute-start.9
  96.1 11.1 %collective-permute-start.12 = (f32[1,1,4,2,4,128]{5,4,3,2,1,0:T(4,128)S(1)}, f32[1,1,4,2,4,128]{5,4,3,2,1,0:T(4,128)S(1)}, u32[]{:S(2)}, u32[]{:S(2)}) collective-permute-start(f32[1,1,4,2,4,128]{5,4,3,2,1,0:T(4,128)S(1)} %copy.104), channel_id=1, source_target_pairs={{0,32},{32,64},{64,96},{96,128},{128,160},{160,192},{192,224},{1,3... | collective-permute-start | bytes 49160 | tf_op jit(solution)/shard_map/ppermute | solution.py:27
  98.0 14.1 %collective-permute-start.15 = (f32[1,1,4,2,4,128]{5,4,3,2,1,0:T(4,128)S(1)}, f32[1,1,4,2,4,128]{5,4,3,2,1,0:T(4,128)S(1)}, u32[]{:S(2)}, u32[]{:S(2)}) collective-permute-start(f32[1,1,4,2,4,128]{5,4,3,2,1,0:T(4,128)S(1)} %copy.104), channel_id=1, source_target_pairs={{1,0},{2,1},{3,2},{4,3},{5,4},{6,5},{7,6},{8,7},{9,8},{10,9},{11,1... | collective-permute-start | bytes 49160 | tf_op jit(solution)/shard_map/ppermute | solution.py:28
  103.7 7.7 %collective-permute-start.14 = (f32[1,1,4,2,4,128]{5,4,3,2,1,0:T(4,128)S(1)}, f32[1,1,4,2,4,128]{5,4,3,2,1,0:T(4,128)S(1)}, u32[]{:S(2)}, u32[]{:S(2)}) collective-permute-start(f32[1,1,4,2,4,128]{5,4,3,2,1,0:T(4,128)S(1)} %copy.104), channel_id=1, source_target_pairs={{0,1},{1,2},{2,3},{3,4},{4,5},{5,6},{6,7},{7,8},{8,9},{9,10},{10,1... | collective-permute-start | bytes 49160 | tf_op jit(solution)/shard_map/ppermute | solution.py:27
  105.7 3.1 collective-permute-start.13
  119.2 76.6 %all-reduce.7.cloned.1.call-start = ((), (), s32[]{:S(2)}) async-start(), calls=%async_computation.1 | async-start | bytes 262144 | tf_op jit(solution)/shard_map/psum | solution.py:40
  164.0 80.8 %all-reduce.9.cloned.1.call-start = ((), (), s32[]{:S(2)}) async-start(), calls=%async_computation.2 | async-start | bytes 262144 | tf_op jit(solution)/shard_map/psum | solution.py:40
  195.8 125.3 %all-reduce.11.cloned.1.call-start = ((), (), s32[]{:S(2)}) async-start(), calls=%async_computation.3 | async-start | bytes 262144 | tf_op jit(solution)/shard_map/psum | solution.py:40
  323.0 109.8 %copy-start.11 = (s32[1024]{0:T(1024)S(1)}, s32[1024]{0:T(1024)}, u32[]{:S(2)}) copy-start(s32[1024]{0:T(1024)} %copy-done.10) | copy-start | bytes 12292
  323.0 125.4 %copy-start.9 = (s32[1024]{0:T(1024)S(1)}, s32[1024]{0:T(1024)}, u32[]{:S(2)}) copy-start(s32[1024]{0:T(1024)} %copy-done.8) | copy-start | bytes 12292
  323.0 126.2 %copy-start.7 = (f32[1,1,8,128]{3,2,1,0:T(8,128)S(1)}, f32[1,1,8,128]{3,2,1,0:T(8,128)}, u32[]{:S(2)}) copy-start(f32[1,1,8,128]{3,2,1,0:T(8,128)} %param.15) | copy-start | bytes 12292
  395.9 9.1 %collective-permute-start.16 = (f32[1,1,4,2,4,128]{5,4,3,2,1,0:T(4,128)S(1)}, f32[1,1,4,2,4,128]{5,4,3,2,1,0:T(4,128)S(1)}, u32[]{:S(2)}, u32[]{:S(2)}) collective-permute-start(f32[1,1,4,2,4,128]{5,4,3,2,1,0:T(4,128)S(1)} %copy.113), channel_id=1, source_target_pairs={{0,32},{32,64},{64,96},{96,128},{128,160},{160,192},{192,224},{1,3... | collective-permute-start | bytes 49160 | tf_op jit(solution)/shard_map/ppermute | solution.py:27
  397.1 12.4 %collective-permute-start.19 = (f32[1,1,4,2,4,128]{5,4,3,2,1,0:T(4,128)S(1)}, f32[1,1,4,2,4,128]{5,4,3,2,1,0:T(4,128)S(1)}, u32[]{:S(2)}, u32[]{:S(2)}) collective-permute-start(f32[1,1,4,2,4,128]{5,4,3,2,1,0:T(4,128)S(1)} %copy.113), channel_id=1, source_target_pairs={{1,0},{2,1},{3,2},{4,3},{5,4},{6,5},{7,6},{8,7},{9,8},{10,9},{11,1... | collective-permute-start | bytes 49160 | tf_op jit(solution)/shard_map/ppermute | solution.py:28
  401.8 7.7 %collective-permute-start.18 = (f32[1,1,4,2,4,128]{5,4,3,2,1,0:T(4,128)S(1)}, f32[1,1,4,2,4,128]{5,4,3,2,1,0:T(4,128)S(1)}, u32[]{:S(2)}, u32[]{:S(2)}) collective-permute-start(f32[1,1,4,2,4,128]{5,4,3,2,1,0:T(4,128)S(1)} %copy.113), channel_id=1, source_target_pairs={{0,1},{1,2},{2,3},{3,4},{4,5},{5,6},{6,7},{7,8},{8,9},{9,10},{10,1... | collective-permute-start | bytes 49160 | tf_op jit(solution)/shard_map/ppermute | solution.py:27
  403.7 3.1 collective-permute-start.17
  413.3 9.5 %collective-permute-start.20 = (f32[1,1,4,2,4,128]{5,4,3,2,1,0:T(4,128)S(1)}, f32[1,1,4,2,4,128]{5,4,3,2,1,0:T(4,128)S(1)}, u32[]{:S(2)}, u32[]{:S(2)}) collective-permute-start(f32[1,1,4,2,4,128]{5,4,3,2,1,0:T(4,128)S(1)} %copy.119), channel_id=1, source_target_pairs={{0,32},{32,64},{64,96},{96,128},{128,160},{160,192},{192,224},{1,3... | collective-permute-start | bytes 49160 | tf_op jit(solution)/shard_map/ppermute | solution.py:27
  414.6 12.7 %collective-permute-start.23 = (f32[1,1,4,2,4,128]{5,4,3,2,1,0:T(4,128)S(1)}, f32[1,1,4,2,4,128]{5,4,3,2,1,0:T(4,128)S(1)}, u32[]{:S(2)}, u32[]{:S(2)}) collective-permute-start(f32[1,1,4,2,4,128]{5,4,3,2,1,0:T(4,128)S(1)} %copy.119), channel_id=1, source_target_pairs={{1,0},{2,1},{3,2},{4,3},{5,4},{6,5},{7,6},{8,7},{9,8},{10,9},{11,1... | collective-permute-start | bytes 49160 | tf_op jit(solution)/shard_map/ppermute | solution.py:28
  419.5 7.7 %collective-permute-start.22 = (f32[1,1,4,2,4,128]{5,4,3,2,1,0:T(4,128)S(1)}, f32[1,1,4,2,4,128]{5,4,3,2,1,0:T(4,128)S(1)}, u32[]{:S(2)}, u32[]{:S(2)}) collective-permute-start(f32[1,1,4,2,4,128]{5,4,3,2,1,0:T(4,128)S(1)} %copy.119), channel_id=1, source_target_pairs={{0,1},{1,2},{2,3},{3,4},{4,5},{5,6},{6,7},{7,8},{8,9},{9,10},{10,1... | collective-permute-start | bytes 49160 | tf_op jit(solution)/shard_map/ppermute | solution.py:27
  421.4 3.1 collective-permute-start.21
  433.4 10.3 %collective-permute-start.24 = (f32[1,1,4,4,4,128]{5,4,3,2,1,0:T(4,128)S(1)}, f32[1,1,4,4,4,128]{5,4,3,2,1,0:T(4,128)S(1)}, u32[]{:S(2)}, u32[]{:S(2)}) collective-permute-start(f32[1,1,4,4,4,128]{5,4,3,2,1,0:T(4,128)S(1)} %bitcast.468), channel_id=1, source_target_pairs={{0,32},{32,64},{64,96},{96,128},{128,160},{160,192},{192,224},{1,3... | collective-permute-start | bytes 98312 | tf_op jit(solution)/shard_map/ppermute | solution.py:27
  434.7 13.7 %collective-permute-start.27 = (f32[1,1,4,4,4,128]{5,4,3,2,1,0:T(4,128)S(1)}, f32[1,1,4,4,4,128]{5,4,3,2,1,0:T(4,128)S(1)}, u32[]{:S(2)}, u32[]{:S(2)}) collective-permute-start(f32[1,1,4,4,4,128]{5,4,3,2,1,0:T(4,128)S(1)} %bitcast.469), channel_id=1, source_target_pairs={{1,0},{2,1},{3,2},{4,3},{5,4},{6,5},{7,6},{8,7},{9,8},{10,9},{11,1... | collective-permute-start | bytes 98312 | tf_op jit(solution)/shard_map/ppermute | solution.py:28
  440.5 7.9 %collective-permute-start.26 = (f32[1,1,4,4,4,128]{5,4,3,2,1,0:T(4,128)S(1)}, f32[1,1,4,4,4,128]{5,4,3,2,1,0:T(4,128)S(1)}, u32[]{:S(2)}, u32[]{:S(2)}) collective-permute-start(f32[1,1,4,4,4,128]{5,4,3,2,1,0:T(4,128)S(1)} %bitcast.470), channel_id=1, source_target_pairs={{0,1},{1,2},{2,3},{3,4},{4,5},{5,6},{6,7},{7,8},{8,9},{9,10},{10,1... | collective-permute-start | bytes 98312 | tf_op jit(solution)/shard_map/ppermute | solution.py:27
  442.4 3.1 collective-permute-start.25
  458.0 10.3 %collective-permute-start.28 = (f32[1,1,4,4,4,128]{5,4,3,2,1,0:T(4,128)S(1)}, f32[1,1,4,4,4,128]{5,4,3,2,1,0:T(4,128)S(1)}, u32[]{:S(2)}, u32[]{:S(2)}) collective-permute-start(f32[1,1,4,4,4,128]{5,4,3,2,1,0:T(4,128)S(1)} %bitcast.464), channel_id=1, source_target_pairs={{0,32},{32,64},{64,96},{96,128},{128,160},{160,192},{192,224},{1,3... | collective-permute-start | bytes 98312 | tf_op jit(solution)/shard_map/ppermute | solution.py:27
  459.3 13.5 %collective-permute-start.31 = (f32[1,1,4,4,4,128]{5,4,3,2,1,0:T(4,128)S(1)}, f32[1,1,4,4,4,128]{5,4,3,2,1,0:T(4,128)S(1)}, u32[]{:S(2)}, u32[]{:S(2)}) collective-permute-start(f32[1,1,4,4,4,128]{5,4,3,2,1,0:T(4,128)S(1)} %bitcast.465), channel_id=1, source_target_pairs={{1,0},{2,1},{3,2},{4,3},{5,4},{6,5},{7,6},{8,7},{9,8},{10,9},{11,1... | collective-permute-start | bytes 98312 | tf_op jit(solution)/shard_map/ppermute | solution.py:28
  464.9 7.9 %collective-permute-start.30 = (f32[1,1,4,4,4,128]{5,4,3,2,1,0:T(4,128)S(1)}, f32[1,1,4,4,4,128]{5,4,3,2,1,0:T(4,128)S(1)}, u32[]{:S(2)}, u32[]{:S(2)}) collective-permute-start(f32[1,1,4,4,4,128]{5,4,3,2,1,0:T(4,128)S(1)} %bitcast.466), channel_id=1, source_target_pairs={{0,1},{1,2},{2,3},{3,4},{4,5},{5,6},{6,7},{7,8},{8,9},{9,10},{10,1... | collective-permute-start | bytes 98312 | tf_op jit(solution)/shard_map/ppermute | solution.py:27
  466.8 3.1 collective-permute-start.29
Sparse Core Ops, SparseCore 0:
  119.3 44.6 all-reduce.4
  166.5 29.1 all-reduce.6
  198.1 46.6 all-reduce.8
  247.0 74.1 all-reduce.10
where the time goes:
time: 491 us; the launch traced here: 489 us
  waiting for transfers between devices  231 us (47%)
  starting transfers between devices  87.9 us (18%)
  blocking collectives  70 us (14%)
  matrix products  53.4 us (11%)
  local copies, waits for them, and re-layouts  26.7 us (5%)
  between operations  13.6 us (3%)
  other arithmetic  6.11 us (1%)
    psum x4, waiting for transfers between devices, by_axis(): return functools.reduce(lax.psum, axes, value)  202 us
    all_gather x1, blocking collectives, on_device(): coarse_x = lax.all_gather(own_rows, ROW_COL, axis=1, tiled=True)  70 us
    ppermute x16, starting transfers between devices, extended_2(): lax.ppermute(leading, axis, [(b, a) for a, b in up])  56.7 us
    dot_general x8, matrix products, apply_op(): coupled = jnp.einsum('bkij,bkrj->bri', blocks, nearby, precision=HIGH)  44.6 us
    ppermute x16, starting transfers between devices, extended_2(): lax.ppermute(last, axis, up)  31.1 us
    ppermute x16, waiting for transfers between devices, extended_2(): lax.ppermute(last, axis, up)  18.3 us
    ppermute x16, waiting for transfers between devices, extended_2(): lax.ppermute(leading, axis, [(b, a) for a, b in up])  11.1 us
  transfers between devices with their start and end apart: 36, of which 19 were waited for; matrix products, arithmetic and copies ran while one was open for 1% of the time, Pallas kernels for 0%

commit v1 on v0

v1 whole, which is shorter than its diff:
```python
import jax
import jax.numpy as jnp
from jax import lax
from jax.experimental import pallas as pl
from jax.experimental.pallas import tpu as pltpu
from jax.sharding import Mesh
from jax.sharding import PartitionSpec as P

OMEGA = 0.3
NX, NC, NY, NZ = 4, 2, 4, 8
BS = 128
NB, NB1, K, G0, G1, R = 8, 2, 14, 4, 2, 4
F32, BF16 = jnp.float32, jnp.bfloat16
MESH = pl.DeviceIdType.MESH
NT = (((1,), (1,)), ((), ()))
NN = (((1,), (0,)), ((), ()))


def split(v):
    hi = v.astype(BF16)
    lo = (v - hi.astype(F32)).astype(BF16)
    return hi, lo


def halves(v):
    hi = v.astype(BF16).astype(F32)
    return hi, v - hi


def eight(v):
    hi, lo = halves(v)
    return jnp.concatenate([hi, lo], axis=0).astype(BF16)


def fold(out):
    n = out.shape[1] // 2
    return (out[0:4, :n] + out[0:4, n:]) + (out[4:8, :n] + out[4:8, n:])


def dot(a, b, dims):
    return lax.dot_general(a, b, dims, preferred_element_type=F32)


def kernel(
    cols0, sends0, agg0, cols1, sends1, agg1,
    rhs, diag0, diag1, blocks0, pro0, blocks1, pro1, cinv,
    out,
    land0, land_p0, land1, land_p1, cin,
    w0, p0, w1, p1,
    ext0, ext1, x0, r0, x1, b1, pack0, ghost0, pack1, ghost1,
    osend, oz, oy, ot, dsend, dz, dy, xsend, xg, crhs, ez, ey, ef,
    lsem, gs, gr, ozs, ozr, oys, oyr, dzs, dzr, dys, dyr, xs, xr, ezs, ezr, eys, eyr, efs, efr, cs, cr,
    unroll,
):
    x, c, y, z = (lax.axis_index(a) for a in ("x", "c", "y", "z"))
    row = x * NC + c
    col = y * NZ + z
    loads = []

    def load(i, src, dst):
        copy = pltpu.make_async_copy(src, dst, lsem.at[i])
        copy.start()
        loads.append(copy)

    for b in range(NB):
        load(b, blocks0.at[0, 0, b], land0.at[b])
    load(NB, pro0.at[0, 0], land_p0)
    load(NB + 1, blocks1.at[0, 0], land1)
    load(NB + 2, pro1.at[0, 0], land_p1)
    load(NB + 3, cinv, cin.at[c])

    def by_row(r):
        r = lax.rem(r + 8, 8)
        return (lax.div(r, 2), lax.rem(r, 2), y, z)

    def by_col(q):
        q = lax.rem(q + 32, 32)
        return (x, c, lax.div(q, NZ), lax.rem(q, NZ))

    near = [by_row(row + 1), by_row(row - 1), by_col(col + 1), by_col(col - 1)]
    valid = [row > 0, row < 7, col > 0, col < 31]
    me_zc = z * 2 + c
    me_xc = row

    def zc_peer(k):
        t = lax.rem(me_zc + k, 16)
        return (x, lax.rem(t, 2), y, lax.div(t, 2))

    def z_peer(k):
        return (x, c, y, lax.rem(z + k, NZ))

    def y_peer(k):
        return (x, c, lax.rem(y + k, NY), z)

    def x_peer(k):
        return (lax.rem(x + k, NX), c, y, z)

    def xc_peer(k):
        t = lax.rem(me_xc + k, 8)
        return (lax.div(t, 2), lax.rem(t, 2), y, z)

    barrier = pltpu.get_barrier_semaphore()
    peers = near + [zc_peer(k) for k in range(1, 16)] + [y_peer(k) for k in range(1, 4)] + [xc_peer(k) for k in range(1, 8)]
    for peer in peers:
        pl.semaphore_signal(barrier, inc=1, device_id=peer, device_id_type=MESH)

    sent = []

    def send(src, dst, ssem, rsem, peer):
        copy = pltpu.make_async_remote_copy(
            src_ref=src, dst_ref=dst, send_sem=ssem, recv_sem=rsem, device_id=peer, device_id_type=MESH
        )
        copy.start()
        sent.append(copy)

    def arrive(dst, ssem, rsem):
        pltpu.make_async_remote_copy(
            src_ref=dst, dst_ref=dst, send_sem=ssem, recv_sem=rsem, device_id=(x, c, y, z), device_id_type=MESH
        ).wait_recv()

    def start_exchange(e, value, sends, pack, ghost, width, base):
        for d in range(4):
            for g in range(width):
                pack[e, d, g] = value[sends[d * width + g]]
        for d in range(4):
            send(pack.at[e, d], ghost.at[e, d], gs.at[base + e, d], gr.at[base + e, d], near[d])

    def own_part(value, ext, count):
        for b in range(count):
            hi, lo = halves(value[b])
            ext[b, 0:4] = hi
            ext[b, 4:8] = lo

    def end_exchange(e, ghost, ext, width, base, count):
        for d in range(4):
            arrive(ghost.at[e, d], gs.at[base + e, d], gr.at[base + e, d])
            for g in range(width):
                hi, lo = halves(jnp.where(valid[d], ghost[e, d, g], 0.0))
                ext[count + d * width + g, 0:4] = hi
                ext[count + d * width + g, 4:8] = lo

    def coupled(b, ext, cols, w):
        v = jnp.concatenate([ext[cols[b * K + k]] for k in range(K)], axis=1).astype(BF16)
        return fold(dot(v, w[b], NT))

    def each(count, body):
        if unroll >= count:
            for b in range(count):
                body(b)
        else:
            def step(t, carry):
                for u in range(unroll):
                    body(t * unroll + u)
                return carry
            lax.fori_loop(0, count // unroll, step, 0)

    def sweep(right, diag, value, ext, cols, w, count):
        def body(b):
            d = diag[b]
            v = value[b]
            value[b] = v + OMEGA * (right[b] - (d * v + coupled(b, ext, cols, w))) / d
        each(count, body)

    def residual(right, diag, value, ext, cols, w, count, res):
        def body(b):
            res[b] = right[b] - (diag[b] * value[b] + coupled(b, ext, cols, w))
        each(count, body)

    class First:
        def __init__(self, ref, vector):
            self.ref, self.vector = ref, vector

        def __getitem__(self, b):
            return self.ref[0, 0, pl.ds(b, 1), :] if self.vector else self.ref[0, 0, b]

    f0, d0, d1 = First(rhs, False), First(diag0, True), First(diag1, True)

    def level0(e):
        start_exchange(e, x0, sends0, pack0, ghost0, G0, 0)

    def level0_end(e):
        own_part(x0, ext0, NB)
        end_exchange(e, ghost0, ext0, G0, 0, NB)

    def level1(e):
        start_exchange(e, x1, sends1, pack1, ghost1, G1, 4)

    def level1_end(e):
        own_part(x1, ext1, NB1)
        end_exchange(e, ghost1, ext1, G1, 4, NB1)

    for b in range(NB):
        x0[b] = OMEGA * f0[b] / d0[b]
    pl.semaphore_wait(barrier, len(peers))
    level0(0)

    lanes = lax.broadcasted_iota(jnp.int32, (2, BS), 1)
    osend[0:2, :] = jnp.where(lanes == agg1[0], 1.0, 0.0)
    osend[2:4, :] = jnp.where(lanes == agg1[1], 1.0, 0.0)
    oz[me_zc] = osend[...]
    for k in (8, 7, 9, 6, 10, 5, 11, 4, 12, 3, 13, 2, 14, 1, 15):
        send(osend, oz.at[me_zc], ozs.at[k], ozr.at[me_zc], zc_peer(k))

    def split0(b, carry):
        pltpu.make_async_copy(blocks0.at[0, 0, b], land0.at[b], lsem.at[b]).wait()
        for k in range(K):
            hi, lo = split(land0[b, k])
            w0[b, 0:BS, k * BS:(k + 1) * BS] = hi
            w0[b, BS:2 * BS, k * BS:(k + 1) * BS] = lo
        return carry

    lax.fori_loop(0, NB, split0, 0)

    level0_end(0)
    sweep(f0, d0, x0, ext0, cols0, w0, NB)
    level0(1)
    own_part(x0, ext0, NB)

    loads[NB].wait()
    for b in range(NB):
        hi, lo = split(land_p0[b])
        p0[b * BS:(b + 1) * BS, 0:BS] = hi
        p0[b * BS:(b + 1) * BS, BS:2 * BS] = lo
    loads[NB + 3].wait()
    send(cin.at[c], cin.at[c], cs, cr, (x, 1 - c, y, z))
    for k in range(1, 16):
        t = lax.rem(me_zc + k, 16)
        arrive(oz.at[t], ozs.at[k], ozr.at[t])
    oy[y] = oz[...]
    for k in (2, 1, 3):
        send(oz, oy.at[y], oys.at[k], oyr.at[y], y_peer(k))

    end_exchange(1, ghost0, ext0, G0, 0, NB)
    residual(f0, d0, x0, ext0, cols0, w0, NB, r0)
    parts = [[], []]
    for b in range(NB):
        both = jnp.concatenate(halves(r0[b]), axis=0)
        for level in range(NB1):
            parts[level].append(jnp.where(agg0[b] == level, both, 0.0))
    lhs = jnp.concatenate([jnp.concatenate(p, axis=1) for p in parts], axis=0).astype(BF16)
    low = dot(lhs, p0[...], NN)
    for level in range(NB1):
        b1[level] = fold(low[level * 8:level * 8 + 8])
        x1[level] = OMEGA * b1[level] / d1[level]
    level1(0)

    loads[NB + 1].wait()
    for b in range(NB1):
        for k in range(K):
            hi, lo = split(land1[b, k])
            w1[b, 0:BS, k * BS:(k + 1) * BS] = hi
            w1[b, BS:2 * BS, k * BS:(k + 1) * BS] = lo
    loads[NB + 2].wait()
    for b in range(NB1):
        hi, lo = split(land_p1[b])
        p1[b, :, 0:BS] = hi
        p1[b, :, BS:2 * BS] = lo
    level1_end(0)
    sweep(b1, d1, x1, ext1, cols1, w1, NB1)
    level1(1)
    own_part(x1, ext1, NB1)

    for k in range(1, 4):
        t = lax.rem(y + k, NY)
        arrive(oy.at[t], oys.at[k], oyr.at[t])
    rows = []
    for q in range(NY):
        for t in range(8):
            rows.append(jnp.concatenate([oy[q, 2 * t], oy[q, 2 * t + 1]], axis=0))
    ot[...] = jnp.concatenate(rows, axis=0).T.astype(BF16)

    end_exchange(1, ghost1, ext1, G1, 4, NB1)
    for b in range(NB1):
        r1 = b1[b] - (d1[b] * x1[b] + coupled(b, ext1, cols1, w1))
        con = fold(dot(eight(r1), p1[b], NN))
        dsend[0, b * 2:b * 2 + 2, :] = con[0:2]
        dsend[1, b * 2:b * 2 + 2, :] = con[2:4]
    dz[me_zc] = dsend[c]
    for k in (8, 7, 9, 6, 10, 5, 11, 4, 12, 3, 13, 2, 14, 1, 15):
        peer = zc_peer(k)
        send(dsend.at[peer[1]], dz.at[me_zc], dzs.at[k], dzr.at[me_zc], peer)
    arrive(cin.at[1 - c], cs, cr)
    for k in range(1, 16):
        t = lax.rem(me_zc + k, 16)
        arrive(dz.at[t], dzs.at[k], dzr.at[t])
    dy[y] = dz[...]
    for k in (2, 1, 3):
        send(dz, dy.at[y], dys.at[k], dyr.at[y], y_peer(k))
    for k in range(1, 4):
        t = lax.rem(y + k, NY)
        arrive(dy.at[t], dys.at[k], dyr.at[t])
    rows = []
    for q in range(NY):
        for t in range(8):
            rows.append(jnp.concatenate([dy[q, 2 * t], dy[q, 2 * t + 1]], axis=0))
    got = jnp.concatenate(rows, axis=0)
    odd = lax.rem(lax.broadcasted_iota(jnp.int32, got.shape, 0), 2)
    ghi, glo = halves(got)
    rhs4 = jnp.concatenate(
        [jnp.where(odd == 0, ghi, 0.0), jnp.where(odd == 1, ghi, 0.0), jnp.where(odd == 0, glo, 0.0), jnp.where(odd == 1, glo, 0.0)],
        axis=1,
    ).astype(BF16)
    dense = dot(ot[...], rhs4, NN)
    xsend[...] = dense[0:64, 0:256] + dense[0:64, 256:512]
    for k in (2, 1, 3):
        send(xsend, xg.at[x], xs.at[k], xr.at[x], x_peer(k))
    total = xsend[...]
    for k in range(1, 4):
        t = lax.rem(x + k, NX)
        arrive(xg.at[t], xs.at[k], xr.at[t])
        total = total + xg[t]
    crhs[0] = total[:, 0:BS]
    crhs[1] = total[:, BS:2 * BS]

    def mat(t, acc):
        acc = list(acc)
        vec = [crhs[r, pl.ds(t, 1), :] for r in range(2)]
        for g in range(2):
            for m in range(4):
                a = cin[g, m * 8:m * 8 + 8, pl.ds(pl.multiple_of(t * BS, BS), BS)]
                for r in range(2):
                    acc[(g * 2 + r) * 4 + m] = acc[(g * 2 + r) * 4 + m] + a * vec[r]
        return tuple(acc)

    acc = lax.fori_loop(0, 64, mat, tuple(jnp.zeros((8, BS), F32) for _ in range(16)), unroll=4)
    zl = lax.rem(z, 4)
    chunks = []
    for q in range(4):
        for part in halves(jnp.concatenate(acc[q * 4:q * 4 + 4], axis=0)):
            chunks.append(jnp.concatenate([jnp.where(zl == s, part, 0.0) for s in range(4)], axis=0))
    place = jnp.concatenate(chunks, axis=1).astype(BF16)
    lhs_row = lax.broadcasted_iota(jnp.int32, (8, 8 * BS), 0)
    lhs_col = lax.div(lax.broadcasted_iota(jnp.int32, (8, 8 * BS), 1), 2 * BS)
    ones = jnp.where(lhs_row == lhs_col, 1.0, 0.0).astype(BF16)
    ez[z] = dot(ones, place, NT)[0:4]
    for k in (4, 3, 5, 2, 6, 1, 7):
        send(ez.at[z], ez.at[z], ezs.at[k], ezr.at[z], z_peer(k))
    for k in range(1, NZ):
        t = lax.rem(z + k, NZ)
        arrive(ez.at[t], ezs.at[k], ezr.at[t])
    for h in range(2):
        ey[y, h] = (ez[4 * h] + ez[4 * h + 1]) + (ez[4 * h + 2] + ez[4 * h + 3])
    for k in (2, 1, 3):
        send(ey.at[y], ey.at[y], eys.at[k], eyr.at[y], y_peer(k))
    for k in range(1, 4):
        t = lax.rem(y + k, NY)
        arrive(ey.at[t], eys.at[k], eyr.at[t])
    for q in range(NY):
        for h in range(2):
            ef[me_xc, q * 2 + h] = ey[q, h]
    for k in (4, 5, 3, 2, 6, 7, 1):
        send(ef.at[me_xc], ef.at[me_xc], efs.at[k], efr.at[me_xc], xc_peer(k))
    for k in range(1, 8):
        t = lax.rem(me_xc + k, 8)
        arrive(ef.at[t], efs.at[k], efr.at[t])
    for b in range(NB1):
        a = agg1[b]
        ax, ag, ayz = lax.div(a, 16), lax.rem(lax.div(a, 8), 2), lax.rem(a, 8)
        half = [ef[ax * 2 + core, ayz] for core in range(2)]
        pick = jnp.concatenate([jnp.where(ag == 0, h[0:2], h[2:4]) for h in half], axis=0)
        e8 = eight(pick)
        o = dot(jnp.concatenate([e8, e8], axis=1), p1[b], NT)
        x1[b] = x1[b] + (o[0:4] + o[4:8])

    for e in (2, 3):
        level1(e)
        level1_end(e)
        sweep(b1, d1, x1, ext1, cols1, w1, NB1)

    for b in range(NB):
        e8 = eight(x1[agg0[b]])
        o = dot(jnp.concatenate([e8, e8], axis=1), p0[b * BS:(b + 1) * BS, :], NT)
        x0[b] = x0[b] + (o[0:4] + o[4:8])
    for e in (2, 3):
        level0(e)
        level0_end(e)
        sweep(f0, d0, x0, ext0, cols0, w0, NB)
    for b in range(NB):
        out[0, 0, b] = x0[b]
    for copy in sent:
        copy.wait_send()


def on_device(rhs, diag0, blocks0, cols0, sends0, pro0, agg0, diag1, blocks1, cols1, sends1, pro1, agg1, cinv, unroll=8):
    vmem = pl.BlockSpec(memory_space=pltpu.VMEM)
    smem = pl.BlockSpec(memory_space=pltpu.SMEM)
    hbm = pl.BlockSpec(memory_space=pl.ANY)
    V = pltpu.VMEM
    dma = pltpu.SemaphoreType.DMA
    scratch = [
        V((NB, K, BS, BS), F32), V((NB, BS, BS), F32), V((NB1, K, BS, BS), F32), V((NB1, BS, BS), F32), V((2, 32, 8192), F32),
        V((NB, 2 * BS, K * BS), BF16), V((NB * BS, 2 * BS), BF16), V((NB1, 2 * BS, K * BS), BF16), V((NB1, BS, 2 * BS), BF16),
        V((NB + 4 * G0, 8, BS), F32), V((NB1 + 4 * G1, 8, BS), F32),
        V((NB, R, BS), F32), V((NB, R, BS), F32), V((NB1, R, BS), F32), V((NB1, R, BS), F32),
        V((4, 4, G0, R, BS), F32), V((4, 4, G0, R, BS), F32), V((4, 4, G1, R, BS), F32), V((4, 4, G1, R, BS), F32),
        V((4, BS), F32), V((16, 4, BS), F32), V((4, 16, 4, BS), F32), V((BS, 256), BF16),
        V((2, 4, BS), F32), V((16, 4, BS), F32), V((4, 16, 4, BS), F32),
        V((64, 256), F32), V((4, 64, 256), F32), V((2, 64, BS), F32),
        V((8, 4, BS), F32), V((4, 2, 4, BS), F32), V((8, 8, 4, BS), F32),
        dma((NB + 4,)), dma((8, 4)), dma((8, 4)),
        dma((16,)), dma((16,)), dma((4,)), dma((4,)),
        dma((16,)), dma((16,)), dma((4,)), dma((4,)),
        dma((4,)), dma((4,)), dma((8,)), dma((8,)), dma((4,)), dma((4,)), dma((8,)), dma((8,)),
        dma, dma,
    ]

    def body(*refs):
        kernel(*refs, unroll=unroll)

    return pl.pallas_call(
        body,
        out_shape=jax.ShapeDtypeStruct(rhs.shape, F32),
        in_specs=[smem] * 6 + [vmem] * 3 + [hbm] * 5,
        out_specs=vmem,
        scratch_shapes=scratch,
        compiler_params=pltpu.CompilerParams(collective_id=0, has_side_effects=True, vmem_limit_bytes=60 * 1024 * 1024),
        name="vcycle",
    )(
        cols0.reshape(-1), sends0.reshape(-1), agg0.reshape(-1), cols1.reshape(-1), sends1.reshape(-1), agg1.reshape(-1),
        rhs, diag0, diag1, blocks0, pro0, blocks1, pro1, cinv,
    )


def solution(mesh):
    finer = Mesh(mesh.devices.reshape(NX, NC, NY, NZ), ("x", "c", "y", "z"))
    ROW, COL = ("x", "c"), ("y", "z")
    ranks = (3, 2, 4, 2, 2, 3, 1, 2, 4, 2, 2, 3, 1)
    in_specs = tuple(P(ROW, COL, *([None] * n)) for n in ranks) + (P(ROW + COL, None),)
    return jax.shard_map(
        on_device, mesh=finer, in_specs=in_specs, out_specs=P(ROW, COL, None, None, None), check_vma=False
    )
```

time: 491 us -> 90.5 us (0.18)
  the two profiles are of different devices: /device:TPU:8 before, /device:TPU:2 now
where the time goes in v1:
time: 90.5 us; the launch traced here: 90.2 us
  Pallas kernels  83.6 us (92%)
  local copies, waits for them, and re-layouts  6.58 us (7%)
    pallas_call x1, Pallas kernels, on_device(): pl.pallas_call(body, out_shape=jax.ShapeDtypeStruct(rhs.shape, F32), in_s...  83.6 us
    unnamed x2, local copies, waits for them, and re-layouts  2.09 us

profile of v1, /device:TPU:2, one launch (start us, length us, event | category | flops | bytes accessed | tf_op | source)
XLA Modules:
  0.0 90.2 jit_solution(12721504784125930137)
XLA Ops:
  0.0 1.3 %reshape.18.refs_0_ = s32[112]{0:T(128)} reshape(s32[1,1,8,14]{3,2,1,0:T(8,128)} %param.17) | data formatting | bytes 896 | tf_op jit(solution)/shard_map/reshape | solution.py:419
  1.3 1.3 %reshape.19.refs_1_ = s32[16]{0:T(128)} reshape(s32[1,1,4,4]{3,2,1,0:T(4,128)} %param.18) | data formatting | bytes 128 | tf_op jit(solution)/shard_map/reshape | solution.py:419
  2.5 1.3 %reshape.21.refs_3_ = s32[28]{0:T(128)} reshape(s32[1,1,2,14]{3,2,1,0:T(2,128)} %param.23) | data formatting | bytes 224 | tf_op jit(solution)/shard_map/reshape | solution.py:419
  3.8 0.8 copy.16
  4.6 0.7 reshape.22.refs_4_
  5.3 83.6 %vcycle.1 = f32[1,1,8,4,128]{4,3,2,1,0:T(4,128)} custom-call(s32[112]{0:T(128)} %reshape.18.refs_0_, s32[16]{0:T(128)} %reshape.19.refs_1_, s32[8]{0:T(128)} %bitcast.4, s32[28]{0:T(128)} %reshape.21.refs_3_, s32[8]{0:T(128)} %reshape.22.refs_4_, s32[2]{0:T(128)} %bitcast.5, f32[1,1,8,4,128]{4,3,2,1,0:T(4,128)} %refs_6_.1, f32[1,1,8,128]{3,2,1,0:T(8,128)} %refs_7_.1, ...), custom_call_target="tpu_custom_call" | custom-call | tf_op jit(solution)/shard_map/vcycle/pallas_call | solution.py:410
  88.9 1.3 %copy.18 = f32[1,1,8,4,128]{4,3,2,1,0:T(4,128)} copy(f32[1,1,8,4,128]{4,3,2,1,0:T(4,128)} %vcycle.1) | data formatting | bytes 32768

commit v2 on v1

v2 whole, which is shorter than its diff:
```python
import jax
import jax.numpy as jnp
from jax import lax
from jax.experimental import pallas as pl
from jax.experimental.pallas import tpu as pltpu
from jax.sharding import Mesh
from jax.sharding import PartitionSpec as P

OMEGA = 0.3
NX, NC, NY, NZ = 4, 2, 4, 8
BS = 128
NB, NB1, K, G0, G1, R = 8, 2, 14, 4, 2, 4
F32, BF16 = jnp.float32, jnp.bfloat16
MESH = pl.DeviceIdType.MESH
NT = (((1,), (1,)), ((), ()))
NN = (((1,), (0,)), ((), ()))


def split(v):
    hi = v.astype(BF16)
    lo = (v - hi.astype(F32)).astype(BF16)
    return hi, lo


def turned(v):
    return jnp.concatenate(split(v.T), axis=1)


def halves(v):
    hi = v.astype(BF16).astype(F32)
    return hi, v - hi


def eight(v):
    hi, lo = halves(v)
    return jnp.concatenate([hi, lo], axis=0).astype(BF16)


def fold(out):
    n = out.shape[1] // 2
    return (out[0:4, :n] + out[0:4, n:]) + (out[4:8, :n] + out[4:8, n:])


def dot(a, b, dims):
    return lax.dot_general(a, b, dims, preferred_element_type=F32)


def kernel(
    cols0, sends0, agg0, cols1, sends1, agg1,
    rhs, diag0, diag1, blocks0, pro0, blocks1, pro1, cinv,
    out,
    rhs_v, diag0_v, diag1_v,
    land0, land_p0, land1, land_p1, cin,
    w0, p0, w1, p1, sel, pp1, gp1, ps1, gsel,
    ext0, ext1, x0, r0, x1, b1, pack0, ghost0, pack1, ghost1,
    osend, oz, oy, ot, dsend, dz, dy, xsend, xg, crhs, ez, ef,
    lsem, gs, gr, ozs, ozr, oys, oyr, dzs, dzr, dys, dyr, xs, xr, ezs, ezr, efs, efr, cs, cr,
    unroll,
):
    x, c, y, z = (lax.axis_index(a) for a in ("x", "c", "y", "z"))
    row = x * NC + c
    col = y * NZ + z
    loads = {}

    def load(i, src, dst):
        copy = pltpu.make_async_copy(src, dst, lsem.at[i])
        copy.start()
        loads[i] = copy

    def by_row(r):
        r = lax.rem(r + 8, 8)
        return (lax.div(r, 2), lax.rem(r, 2), y, z)

    def by_col(q):
        q = lax.rem(q + 32, 32)
        return (x, c, lax.div(q, NZ), lax.rem(q, NZ))

    near = [by_row(row + 1), by_row(row - 1), by_col(col + 1), by_col(col - 1)]
    valid = [row > 0, row < 7, col > 0, col < 31]
    me_zc = z * 2 + c

    def zc_peer(k):
        t = lax.rem(me_zc + k, 16)
        return (x, lax.rem(t, 2), y, lax.div(t, 2))

    def y_peer(k):
        return (x, c, lax.rem(y + k, NY), z)

    def x_peer(k):
        return (lax.rem(x + k, NX), c, y, z)

    me_xy = x * NY + y

    def xy_peer(k):
        return (lax.rem(x + k // 4, NX), c, lax.rem(y + k % 4, NY), z)

    barrier = pltpu.get_barrier_semaphore()
    peers = near + [zc_peer(k) for k in range(1, 16)] + [xy_peer(k) for k in range(1, 16)]
    for peer in peers:
        pl.semaphore_signal(barrier, inc=1, device_id=peer, device_id_type=MESH)

    load(NB + 4, rhs.at[0, 0], rhs_v)
    load(NB + 5, diag0.at[0, 0], diag0_v)
    load(NB + 6, diag1.at[0, 0], diag1_v)
    load(NB + 2, pro1.at[0, 0], land_p1)
    for b in range(NB):
        load(b, blocks0.at[0, 0, b], land0.at[b])
    load(NB, pro0.at[0, 0], land_p0)
    load(NB + 1, blocks1.at[0, 0], land1)
    load(NB + 3, cinv, cin.at[c])
    sent, due = [], {}

    def post(key, src, dst, ssem, rsem, peer, landing, landed):
        copy = pltpu.make_async_remote_copy(
            src_ref=src, dst_ref=dst, send_sem=ssem, recv_sem=rsem, device_id=peer, device_id_type=MESH
        )
        copy.start()
        sent.append(copy)
        due[key] = pltpu.make_async_remote_copy(
            src_ref=landing, dst_ref=landing, send_sem=ssem, recv_sem=landed, device_id=peer, device_id_type=MESH
        )

    def take(*key):
        due.pop(key).wait_recv()


    def start_exchange(e, value, pick, pack, ghost, width, base):
        for d in range(4):
            for g in range(width):
                pack[e, d, g] = value[pick(d, g)]
        for d in range(4):
            sems = gs.at[base + e, d], gr.at[base + e, d]
            post((base + e, d), pack.at[e, d], ghost.at[e, d], *sems, near[d], ghost.at[e, d], sems[1])

    def own_part(value, ext, count):
        for b in range(count):
            hi, lo = halves(value[b])
            ext[b, 0:4] = hi
            ext[b, 4:8] = lo

    def end_exchange(e, ghost, ext, width, base, count):
        for d in range(4):
            take(base + e, d)
            for g in range(width):
                hi, lo = halves(jnp.where(valid[d], ghost[e, d, g], 0.0))
                ext[count + d * width + g, 0:4] = hi
                ext[count + d * width + g, 4:8] = lo

    def coupled(b, ext, cols, w):
        v = jnp.concatenate([ext[cols[0, 0, b, k]] for k in range(K)], axis=1).astype(BF16)
        return fold(dot(v, w[b], NN))

    def each(count, body):
        if unroll >= count:
            for b in range(count):
                body(b)
        else:
            def step(t, carry):
                for u in range(unroll):
                    body(t * unroll + u)
                return carry
            lax.fori_loop(0, count // unroll, step, 0)

    def sweep(right, diag, value, ext, cols, w, count):
        def body(b):
            d = diag[b]
            v = value[b]
            value[b] = v + OMEGA * (right[b] - (d * v + coupled(b, ext, cols, w))) / d
        each(count, body)

    def residual(right, diag, value, ext, cols, w, count, res):
        def body(b):
            res[b] = right[b] - (diag[b] * value[b] + coupled(b, ext, cols, w))
        each(count, body)

    class First:
        def __init__(self, ref, vector):
            self.ref, self.vector = ref, vector

        def __getitem__(self, b):
            return self.ref[pl.ds(b, 1), :] if self.vector else self.ref[b]

    f0, d0, d1 = rhs_v, First(diag0_v, True), First(diag1_v, True)

    def level0(e):
        start_exchange(e, x0, lambda d, g: sends0[0, 0, d, g], pack0, ghost0, G0, 0)

    def level0_end(e):
        own_part(x0, ext0, NB)
        end_exchange(e, ghost0, ext0, G0, 0, NB)

    def level1(e):
        start_exchange(e, x1, lambda d, g: sends1[0, 0, g, d], pack1, ghost1, G1, 4)

    def level1_end(e):
        own_part(x1, ext1, NB1)
        end_exchange(e, ghost1, ext1, G1, 4, NB1)

    for n in (4, 5, 6):
        loads.pop(NB + n).wait()
    for b in range(NB):
        x0[b] = OMEGA * f0[b] / d0[b]
    pl.semaphore_wait(barrier, len(peers))
    level0(0)

    loads.pop(NB + 2).wait()
    spot = lax.broadcasted_iota(jnp.int32, (4, 256), 1)
    rr = lax.broadcasted_iota(jnp.int32, (4, 256), 0)

    def rows_of(a):
        ax, ag, ay, ah = lax.div(a, 16), lax.rem(lax.div(a, 8), 2), lax.rem(lax.div(a, 2), 4), lax.rem(a, 2)
        base = (ax * 4 + ay) * 16 + ah * 4 + ag * 2
        return jnp.where(spot == base + lax.div(rr, 2) * 8 + lax.rem(rr, 2), 1.0, 0.0)

    for d in range(4):
        for g in range(G1):
            pp1[d, g] = land_p1[sends1[0, 0, g, d]]
            ps1[d, g] = rows_of(agg1[0, 0, sends1[0, 0, g, d]])
    for d in range(4):
        post(("pp", d), pp1.at[d], gp1.at[d], gs.at[8, d], gr.at[8, d], near[d], gp1.at[d], gr.at[8, d])
        post(("ps", d), ps1.at[d], gsel.at[d], gs.at[9, d], gr.at[9, d], near[d], gsel.at[d], gr.at[9, d])
    lanes = lax.broadcasted_iota(jnp.int32, (2, BS), 1)
    osend[0:2, :] = jnp.where(lanes == agg1[0, 0, 0], 1.0, 0.0)
    osend[2:4, :] = jnp.where(lanes == agg1[0, 0, 1], 1.0, 0.0)
    oz[me_zc] = osend[...]
    for k in (8, 7, 9, 6, 10, 5, 11, 4, 12, 3, 13, 2, 14, 1, 15):
        t = lax.rem(me_zc + k, 16)
        post(("oz", k), osend, oz.at[me_zc], ozs.at[k], ozr.at[me_zc], zc_peer(k), oz.at[t], ozr.at[t])

    def split0(b, carry):
        pltpu.make_async_copy(blocks0.at[0, 0, b], land0.at[b], lsem.at[b]).wait()
        for k in range(K):
            w0[b, k * BS:(k + 1) * BS, :] = turned(land0[b, k])
        return carry

    lax.fori_loop(0, NB, split0, 0)
    for b in range(NB):
        loads.pop(b)

    level0_end(0)
    sweep(f0, d0, x0, ext0, cols0, w0, NB)
    level0(1)
    own_part(x0, ext0, NB)

    loads.pop(NB).wait()
    for b in range(NB):
        hi, lo = split(land_p0[b])
        p0[b * BS:(b + 1) * BS, 0:BS] = hi
        p0[b * BS:(b + 1) * BS, BS:2 * BS] = lo
    loads.pop(NB + 3).wait()
    post(("cin",), cin.at[c], cin.at[c], cs, cr, (x, 1 - c, y, z), cin.at[1 - c], cr)
    for k in range(1, 16):
        take("oz", k)
    oy[y] = oz[...]
    for k in (2, 1, 3):
        t = lax.rem(y + k, NY)
        post(("oy", k), oz, oy.at[y], oys.at[k], oyr.at[y], y_peer(k), oy.at[t], oyr.at[t])

    end_exchange(1, ghost0, ext0, G0, 0, NB)
    residual(f0, d0, x0, ext0, cols0, w0, NB, r0)
    parts = [[], []]
    for b in range(NB):
        both = jnp.concatenate(halves(r0[b]), axis=0)
        for level in range(NB1):
            parts[level].append(jnp.where(agg0[0, 0, b] == level, both, 0.0))
    lhs = jnp.concatenate([jnp.concatenate(p, axis=1) for p in parts], axis=0).astype(BF16)
    low = dot(lhs, p0[...], NN)
    for level in range(NB1):
        b1[level] = fold(low[level * 8:level * 8 + 8])
        x1[level] = OMEGA * b1[level] / d1[level]
    level1(0)

    loads.pop(NB + 1).wait()
    for b in range(NB1):
        for k in range(K):
            w1[b, k * BS:(k + 1) * BS, :] = turned(land1[b, k])
    for b in range(NB1):
        hi, lo = split(land_p1[b])
        p1[b, :, 0:BS] = hi
        p1[b, :, BS:2 * BS] = lo
        sel[b * 4:b * 4 + 4, :] = rows_of(agg1[0, 0, b]).astype(BF16)
    for d in range(4):
        take("pp", d)
        take("ps", d)
        for g in range(G1):
            n = NB1 + d * G1 + g
            hi, lo = split(gp1[d, g])
            p1[n, :, 0:BS] = hi
            p1[n, :, BS:2 * BS] = lo
            sel[n * 4:n * 4 + 4, :] = jnp.where(valid[d], gsel[d, g], 0.0).astype(BF16)
    level1_end(0)
    sweep(b1, d1, x1, ext1, cols1, w1, NB1)
    level1(1)
    own_part(x1, ext1, NB1)

    for k in range(1, 4):
        take("oy", k)
    rows = []
    for q in range(NY):
        for t in range(8):
            rows.append(jnp.concatenate([oy[q, 2 * t], oy[q, 2 * t + 1]], axis=0))
    ot[...] = jnp.concatenate(rows, axis=0).T.astype(BF16)

    end_exchange(1, ghost1, ext1, G1, 4, NB1)
    for b in range(NB1):
        r1 = b1[b] - (d1[b] * x1[b] + coupled(b, ext1, cols1, w1))
        con = fold(dot(eight(r1), p1[b], NN))
        dsend[0, b * 2:b * 2 + 2, :] = con[0:2]
        dsend[1, b * 2:b * 2 + 2, :] = con[2:4]
    dz[me_zc] = dsend[c]
    for k in (8, 7, 9, 6, 10, 5, 11, 4, 12, 3, 13, 2, 14, 1, 15):
        peer = zc_peer(k)
        t = lax.rem(me_zc + k, 16)
        post(("dz", k), dsend.at[peer[1]], dz.at[me_zc], dzs.at[k], dzr.at[me_zc], peer, dz.at[t], dzr.at[t])
    take("cin")
    for k in range(1, 16):
        take("dz", k)
    dy[y] = dz[...]
    for k in (2, 1, 3):
        t = lax.rem(y + k, NY)
        post(("dy", k), dz, dy.at[y], dys.at[k], dyr.at[y], y_peer(k), dy.at[t], dyr.at[t])
    for k in range(1, 4):
        take("dy", k)
    rows = []
    for q in range(NY):
        for t in range(8):
            rows.append(jnp.concatenate([dy[q, 2 * t], dy[q, 2 * t + 1]], axis=0))
    got = jnp.concatenate(rows, axis=0)
    odd = lax.rem(lax.broadcasted_iota(jnp.int32, got.shape, 0), 2)
    ghi, glo = halves(got)
    rhs4 = jnp.concatenate(
        [jnp.where(odd == 0, ghi, 0.0), jnp.where(odd == 1, ghi, 0.0), jnp.where(odd == 0, glo, 0.0), jnp.where(odd == 1, glo, 0.0)],
        axis=1,
    ).astype(BF16)
    dense = dot(ot[...], rhs4, NN)
    xsend[...] = dense[0:64, 0:256] + dense[0:64, 256:512]
    for k in (2, 1, 3):
        t = lax.rem(x + k, NX)
        post(("x", k), xsend, xg.at[x], xs.at[k], xr.at[x], x_peer(k), xg.at[t], xr.at[t])
    total = xsend[...]
    for k in range(1, 4):
        t = lax.rem(x + k, NX)
        take("x", k)
        total = total + xg[t]
    crhs[0] = total[:, 0:BS]
    crhs[1] = total[:, BS:2 * BS]

    def mat(t, acc):
        acc = list(acc)
        vec = [crhs[r, pl.ds(t, 1), :] for r in range(2)]
        for g in range(2):
            for m in range(4):
                a = cin[g, m * 8:m * 8 + 8, pl.ds(pl.multiple_of(t * BS, BS), BS)]
                for r in range(2):
                    acc[(g * 2 + r) * 4 + m] = acc[(g * 2 + r) * 4 + m] + a * vec[r]
        return tuple(acc)

    acc = lax.fori_loop(0, 64, mat, tuple(jnp.zeros((8, BS), F32) for _ in range(16)), unroll=4)
    zl = lax.rem(z, 4)
    chunks = []
    for q in range(4):
        for part in halves(jnp.concatenate(acc[q * 4:q * 4 + 4], axis=0)):
            chunks.append(jnp.concatenate([jnp.where(zl == s, part, 0.0) for s in range(4)], axis=0))
    place = jnp.concatenate(chunks, axis=1).astype(BF16)
    lhs_row = lax.broadcasted_iota(jnp.int32, (8, 8 * BS), 0)
    lhs_col = lax.div(lax.broadcasted_iota(jnp.int32, (8, 8 * BS), 1), 2 * BS)
    ones = jnp.where(lhs_row == lhs_col, 1.0, 0.0).astype(BF16)
    ez[me_zc] = dot(ones, place, NT)[0:4]
    for k in (8, 7, 9, 6, 10, 5, 11, 4, 12, 3, 13, 2, 14, 1, 15):
        t = lax.rem(me_zc + k, 16)
        post(("ez", k), ez.at[me_zc], ez.at[me_zc], ezs.at[k], ezr.at[me_zc], zc_peer(k), ez.at[t], ezr.at[t])
    for k in range(1, 16):
        take("ez", k)
    for h in range(2):
        for core in range(2):
            n = [ez[(4 * h + q) * 2 + core] for q in range(4)]
            ef[me_xy, core * 2 + h] = (n[0] + n[1]) + (n[2] + n[3])
    for k in (10, 9, 11, 6, 14, 2, 8, 5, 7, 13, 15, 1, 3, 4, 12):
        t = xy_peer(k)
        n = t[0] * NY + t[2]
        post(("ef", k), ef.at[me_xy], ef.at[me_xy], efs.at[k], efr.at[me_xy], t, ef.at[n], efr.at[n])
    for k in range(1, 16):
        take("ef", k)
    every = jnp.concatenate(
        [jnp.concatenate([ef[n, 2 * m], ef[n, 2 * m + 1]], axis=0) for n in range(16) for m in range(2)], axis=0
    )
    both = dot(sel[...], jnp.concatenate(split(every), axis=1), NN)
    picked = both[:, 0:BS] + both[:, BS:2 * BS]
    for n in range(NB1 + 4 * G1):
        e8 = eight(picked[n * 4:n * 4 + 4])
        o = dot(jnp.concatenate([e8, e8], axis=1), p1[n], NT)
        o = o[0:4] + o[4:8]
        if n < NB1:
            x1[n] = x1[n] + o
        else:
            hi, lo = halves(ext1[n, 0:4] + ext1[n, 4:8] + o)
            ext1[n, 0:4] = hi
            ext1[n, 4:8] = lo
    own_part(x1, ext1, NB1)
    for e in (2, 3):
        if e == 3:
            level1(e)
            level1_end(e)
        sweep(b1, d1, x1, ext1, cols1, w1, NB1)

    for b in range(NB):
        e8 = eight(x1[agg0[0, 0, b]])
        o = dot(jnp.concatenate([e8, e8], axis=1), p0[b * BS:(b + 1) * BS, :], NT)
        x0[b] = x0[b] + (o[0:4] + o[4:8])
    for e in (2, 3):
        level0(e)
        level0_end(e)
        sweep(f0, d0, x0, ext0, cols0, w0, NB)
    for b in range(NB):
        out[0, 0, b] = x0[b]
    for copy in sent:
        copy.wait_send()


def on_device(rhs, diag0, blocks0, cols0, sends0, pro0, agg0, diag1, blocks1, cols1, sends1, pro1, agg1, cinv, unroll=8):
    vmem = pl.BlockSpec(memory_space=pltpu.VMEM)
    smem = pl.BlockSpec(memory_space=pltpu.SMEM)
    hbm = pl.BlockSpec(memory_space=pl.ANY)
    V = pltpu.VMEM
    dma = pltpu.SemaphoreType.DMA
    scratch = [
        V((NB, R, BS), F32), V((NB, BS), F32), V((NB1, BS), F32),
        V((NB, K, BS, BS), F32), V((NB, BS, BS), F32), V((NB1, K, BS, BS), F32), V((NB1, BS, BS), F32), V((2, 32, 8192), F32),
        V((NB, K * BS, 2 * BS), BF16), V((NB * BS, 2 * BS), BF16), V((NB1, K * BS, 2 * BS), BF16), V((NB1 + 4 * G1, BS, 2 * BS), BF16), V((40, 256), BF16),
        V((4, G1, BS, BS), F32), V((4, G1, BS, BS), F32), V((4, G1, 4, 256), F32), V((4, G1, 4, 256), F32),
        V((NB + 4 * G0, 8, BS), F32), V((NB1 + 4 * G1, 8, BS), F32),
        V((NB, R, BS), F32), V((NB, R, BS), F32), V((NB1, R, BS), F32), V((NB1, R, BS), F32),
        V((4, 4, G0, R, BS), F32), V((4, 4, G0, R, BS), F32), V((4, 4, G1, R, BS), F32), V((4, 4, G1, R, BS), F32),
        V((4, BS), F32), V((16, 4, BS), F32), V((4, 16, 4, BS), F32), V((BS, 256), BF16),
        V((2, 4, BS), F32), V((16, 4, BS), F32), V((4, 16, 4, BS), F32),
        V((64, 256), F32), V((4, 64, 256), F32), V((2, 64, BS), F32),
        V((16, 4, BS), F32), V((16, 4, 4, BS), F32),
        dma((NB + 7,)), dma((10, 4)), dma((10, 4)),
        dma((16,)), dma((16,)), dma((4,)), dma((4,)),
        dma((16,)), dma((16,)), dma((4,)), dma((4,)),
        dma((4,)), dma((4,)), dma((16,)), dma((16,)), dma((16,)), dma((16,)),
        dma, dma,
    ]

    def body(*refs):
        kernel(*refs, unroll=unroll)

    return pl.pallas_call(
        body,
        out_shape=jax.ShapeDtypeStruct(rhs.shape, F32),
        in_specs=[smem] * 6 + [hbm] * 8,
        out_specs=vmem,
        scratch_shapes=scratch,
        compiler_params=pltpu.CompilerParams(collective_id=0, has_side_effects=True, vmem_limit_bytes=60 * 1024 * 1024),
        name="vcycle",
    )(
        cols0, sends0, agg0, cols1, sends1.transpose(0, 1, 3, 2), agg1,
        rhs, diag0, diag1, blocks0, pro0, blocks1, pro1, cinv,
    )


def solution(mesh):
    finer = Mesh(mesh.devices.reshape(NX, NC, NY, NZ), ("x", "c", "y", "z"))
    ROW, COL = ("x", "c"), ("y", "z")
    ranks = (3, 2, 4, 2, 2, 3, 1, 2, 4, 2, 2, 3, 1)
    in_specs = tuple(P(ROW, COL, *([None] * n)) for n in ranks) + (P(ROW + COL, None),)
    return jax.shard_map(
        on_device, mesh=finer, in_specs=in_specs, out_specs=P(ROW, COL, None, None, None), check_vma=False
    )
```

time: 90.5 us -> 74.3 us (0.82)
  Pallas kernels: 83.6 us -> 72.7 us
  local copies, waits for them, and re-layouts: 6.58 us -> 1.32 us
    pallas_call x1, Pallas kernels: 83.6 us -> 72.7 us  [on_device(): pl.pallas_call(body, out_shape=jax.ShapeDtypeStruct(rhs.shape, F32), in_s...]
    reshape x4 -> x0, local copies, waits for them, and re-layouts: 4.5 us -> none  [the longest x1 1.29 us: on_device(): cols1.reshape(-1)]
    unnamed x2 -> x1, local copies, waits for them, and re-layouts: 2.09 us -> 1.32 us
where the time goes in v2:
time: 74.3 us; the launch traced here: 74 us
  Pallas kernels  72.7 us (98%)
  local copies, waits for them, and re-layouts  1.32 us (2%)
    pallas_call x1, Pallas kernels, on_device(): pl.pallas_call(body, out_shape=jax.ShapeDtypeStruct(rhs.shape, F32), in_s...  72.7 us

profile of v2, /device:TPU:2, one launch (start us, length us, event | category | flops | bytes accessed | tf_op | source)
XLA Modules:
  0.0 74.0 jit_solution(2631232155500074944)
XLA Ops:
  0.0 72.7 %vcycle.1 = f32[1,1,8,4,128]{4,3,2,1,0:T(4,128)} custom-call(s32[1,1,8,14]{3,2,1,0:T(8,128)} %refs_0_.1, s32[1,1,4,4]{3,2,1,0:T(4,128)} %refs_1_.1, s32[1,1,8]{2,1,0:T(1,128)} %refs_2_.1, s32[1,1,2,14]{3,2,1,0:T(2,128)} %refs_3_.1, s32[1,1,2,4]{3,2,1,0:T(2,128)} %bitcast.1, s32[1,1,2]{2,1,0:T(1,128)} %refs_5_.1, f32[1,1,8,4,128]{4,3,2,1,0:T(4,128)} %refs_6_.1, ...), custom_call_target="tpu_custom_call" | custom-call | tf_op jit(solution)/shard_map/vcycle/pallas_call | solution.py:448
  72.7 1.3 %copy.16 = f32[1,1,8,4,128]{4,3,2,1,0:T(4,128)} copy(f32[1,1,8,4,128]{4,3,2,1,0:T(4,128)} %vcycle.1) | data formatting | bytes 32768

commit v3 on v2

--- a/solution.py
+++ b/solution.py
@@ -22,8 +22,9 @@
     return hi, lo
 
 
-def turned(v):
-    return jnp.concatenate(split(v.T), axis=1)
+def turned(eye, left, right):
+    both = [jnp.concatenate(pair, axis=1) for pair in zip(split(left), split(right))]
+    return dot(eye, jnp.concatenate(both, axis=0), NT).astype(BF16)
 
 
 def halves(v):
@@ -46,9 +47,10 @@
 
 
 def kernel(
-    cols0, sends0, agg0, cols1, sends1, agg1,
+    cols0_h, sends0_h, agg0_h, cols1_h, sends1_h, agg1_h,
     rhs, diag0, diag1, blocks0, pro0, blocks1, pro1, cinv,
     out,
+    cols0, sends0, agg0, cols1, sends1, agg1,
     rhs_v, diag0_v, diag1_v,
     land0, land_p0, land1, land_p1, cin,
     w0, p0, w1, p1, sel, pp1, gp1, ps1, gsel,
@@ -77,6 +79,7 @@
 
     near = [by_row(row + 1), by_row(row - 1), by_col(col + 1), by_col(col - 1)]
     valid = [row > 0, row < 7, col > 0, col < 31]
+    reaches = [row < 7, row > 0, col < 31, col > 0]
     me_zc = z * 2 + c
 
     def zc_peer(k):
@@ -99,6 +102,10 @@
     for peer in peers:
         pl.semaphore_signal(barrier, inc=1, device_id=peer, device_id_type=MESH)
 
+    for i, (src, dst) in enumerate(
+        ((sends0_h, sends0), (sends1_h, sends1), (agg1_h, agg1), (cols0_h, cols0), (agg0_h, agg0), (cols1_h, cols1))
+    ):
+        load(NB + 7 + i, src, dst)
     load(NB + 4, rhs.at[0, 0], rhs_v)
     load(NB + 5, diag0.at[0, 0], diag0_v)
     load(NB + 6, diag1.at[0, 0], diag1_v)
@@ -108,7 +115,7 @@
     load(NB, pro0.at[0, 0], land_p0)
     load(NB + 1, blocks1.at[0, 0], land1)
     load(NB + 3, cinv, cin.at[c])
-    sent, due = [], {}
+    sent, sent_near, due = [], [], {}
 
     def post(key, src, dst, ssem, rsem, peer, landing, landed):
         copy = pltpu.make_async_remote_copy(
@@ -123,14 +130,25 @@
     def take(*key):
         due.pop(key).wait_recv()
 
+    def post_near(key, src, dst, ssem, rsem, d):
+        copy = pltpu.make_async_remote_copy(
+            src_ref=src, dst_ref=dst, send_sem=ssem, recv_sem=rsem, device_id=near[d], device_id_type=MESH
+        )
+        pl.when(reaches[d])(copy.start)
+        sent_near.append((d, copy))
+        due[key] = (d, copy)
+
+    def take_near(*key):
+        d, copy = due.pop(key)
+        pl.when(valid[d])(copy.wait_recv)
+
 
     def start_exchange(e, value, pick, pack, ghost, width, base):
         for d in range(4):
             for g in range(width):
                 pack[e, d, g] = value[pick(d, g)]
         for d in range(4):
-            sems = gs.at[base + e, d], gr.at[base + e, d]
-            post((base + e, d), pack.at[e, d], ghost.at[e, d], *sems, near[d], ghost.at[e, d], sems[1])
+            post_near((base + e, d), pack.at[e, d], ghost.at[e, d], gs.at[base + e, d], gr.at[base + e, d], d)
 
     def own_part(value, ext, count):
         for b in range(count):
@@ -140,7 +158,7 @@
 
     def end_exchange(e, ghost, ext, width, base, count):
         for d in range(4):
-            take(base + e, d)
+            take_near(base + e, d)
             for g in range(width):
                 hi, lo = halves(jnp.where(valid[d], ghost[e, d, g], 0.0))
                 ext[count + d * width + g, 0:4] = hi
@@ -196,7 +214,7 @@
         own_part(x1, ext1, NB1)
         end_exchange(e, ghost1, ext1, G1, 4, NB1)
 
-    for n in (4, 5, 6):
+    for n in range(4, 13):
         loads.pop(NB + n).wait()
     for b in range(NB):
         x0[b] = OMEGA * f0[b] / d0[b]
@@ -217,8 +235,8 @@
             pp1[d, g] = land_p1[sends1[0, 0, g, d]]
             ps1[d, g] = rows_of(agg1[0, 0, sends1[0, 0, g, d]])
     for d in range(4):
-        post(("pp", d), pp1.at[d], gp1.at[d], gs.at[8, d], gr.at[8, d], near[d], gp1.at[d], gr.at[8, d])
-        post(("ps", d), ps1.at[d], gsel.at[d], gs.at[9, d], gr.at[9, d], near[d], gsel.at[d], gr.at[9, d])
+        post_near(("pp", d), pp1.at[d], gp1.at[d], gs.at[8, d], gr.at[8, d], d)
+        post_near(("ps", d), ps1.at[d], gsel.at[d], gs.at[9, d], gr.at[9, d], d)
     lanes = lax.broadcasted_iota(jnp.int32, (2, BS), 1)
     osend[0:2, :] = jnp.where(lanes == agg1[0, 0, 0], 1.0, 0.0)
     osend[2:4, :] = jnp.where(lanes == agg1[0, 0, 1], 1.0, 0.0)
@@ -227,10 +245,14 @@
         t = lax.rem(me_zc + k, 16)
         post(("oz", k), osend, oz.at[me_zc], ozs.at[k], ozr.at[me_zc], zc_peer(k), oz.at[t], ozr.at[t])
 
+    eye = jnp.where(
+        lax.broadcasted_iota(jnp.int32, (256, 256), 0) == lax.broadcasted_iota(jnp.int32, (256, 256), 1), 1.0, 0.0
+    ).astype(BF16)
+
     def split0(b, carry):
         pltpu.make_async_copy(blocks0.at[0, 0, b], land0.at[b], lsem.at[b]).wait()
-        for k in range(K):
-            w0[b, k * BS:(k + 1) * BS, :] = turned(land0[b, k])
+        for k in range(0, K, 2):
+            w0[b, k * BS:(k + 2) * BS, :] = turned(eye, land0[b, k], land0[b, k + 1])
         return carry
 
     lax.fori_loop(0, NB, split0, 0)
@@ -272,19 +294,19 @@
 
     loads.pop(NB + 1).wait()
     for b in range(NB1):
-        for k in range(K):
-            w1[b, k * BS:(k + 1) * BS, :] = turned(land1[b, k])
+        for k in range(0, K, 2):
+            w1[b, k * BS:(k + 2) * BS, :] = turned(eye, land1[b, k], land1[b, k + 1])
     for b in range(NB1):
         hi, lo = split(land_p1[b])
         p1[b, :, 0:BS] = hi
         p1[b, :, BS:2 * BS] = lo
         sel[b * 4:b * 4 + 4, :] = rows_of(agg1[0, 0, b]).astype(BF16)
     for d in range(4):
-        take("pp", d)
-        take("ps", d)
+        take_near("pp", d)
+        take_near("ps", d)
         for g in range(G1):
             n = NB1 + d * G1 + g
-            hi, lo = split(gp1[d, g])
+            hi, lo = split(jnp.where(valid[d], gp1[d, g], 0.0))
             p1[n, :, 0:BS] = hi
             p1[n, :, BS:2 * BS] = lo
             sel[n * 4:n * 4 + 4, :] = jnp.where(valid[d], gsel[d, g], 0.0).astype(BF16)
@@ -415,15 +437,19 @@
         out[0, 0, b] = x0[b]
     for copy in sent:
         copy.wait_send()
+    for d, copy in sent_near:
+        pl.when(reaches[d])(copy.wait_send)
 
 
 def on_device(rhs, diag0, blocks0, cols0, sends0, pro0, agg0, diag1, blocks1, cols1, sends1, pro1, agg1, cinv, unroll=8):
     vmem = pl.BlockSpec(memory_space=pltpu.VMEM)
-    smem = pl.BlockSpec(memory_space=pltpu.SMEM)
     hbm = pl.BlockSpec(memory_space=pl.ANY)
     V = pltpu.VMEM
     dma = pltpu.SemaphoreType.DMA
+    S = pltpu.SMEM
+    index = [cols0, sends0, agg0, cols1, sends1.transpose(0, 1, 3, 2), agg1]
     scratch = [
+        *[S(a.shape, jnp.int32) for a in index],
         V((NB, R, BS), F32), V((NB, BS), F32), V((NB1, BS), F32),
         V((NB, K, BS, BS), F32), V((NB, BS, BS), F32), V((NB1, K, BS, BS), F32), V((NB1, BS, BS), F32), V((2, 32, 8192), F32),
         V((NB, K * BS, 2 * BS), BF16), V((NB * BS, 2 * BS), BF16), V((NB1, K * BS, 2 * BS), BF16), V((NB1 + 4 * G1, BS, 2 * BS), BF16), V((40, 256), BF16),
@@ -435,7 +461,7 @@
         V((2, 4, BS), F32), V((16, 4, BS), F32), V((4, 16, 4, BS), F32),
         V((64, 256), F32), V((4, 64, 256), F32), V((2, 64, BS), F32),
         V((16, 4, BS), F32), V((16, 4, 4, BS), F32),
-        dma((NB + 7,)), dma((10, 4)), dma((10, 4)),
+        dma((NB + 13,)), dma((10, 4)), dma((10, 4)),
         dma((16,)), dma((16,)), dma((4,)), dma((4,)),
         dma((16,)), dma((16,)), dma((4,)), dma((4,)),
         dma((4,)), dma((4,)), dma((16,)), dma((16,)), dma((16,)), dma((16,)),
@@ -448,14 +474,13 @@
     return pl.pallas_call(
         body,
         out_shape=jax.ShapeDtypeStruct(rhs.shape, F32),
-        in_specs=[smem] * 6 + [hbm] * 8,
+        in_specs=[hbm] * 14,
         out_specs=vmem,
         scratch_shapes=scratch,
         compiler_params=pltpu.CompilerParams(collective_id=0, has_side_effects=True, vmem_limit_bytes=60 * 1024 * 1024),
         name="vcycle",
     )(
-        cols0, sends0, agg0, cols1, sends1.transpose(0, 1, 3, 2), agg1,
-        rhs, diag0, diag1, blocks0, pro0, blocks1, pro1, cinv,
+        *index, rhs, diag0, diag1, blocks0, pro0, blocks1, pro1, cinv,
     )
 
 

time: 74.3 us -> 70.9 us (0.954)
  the two profiles are of different devices: /device:TPU:2 before, /device:TPU:8 now
where the time goes in v3:
time: 70.9 us; the launch traced here: 70.7 us
  Pallas kernels  69.4 us (98%)
  local copies, waits for them, and re-layouts  1.32 us (2%)
    pallas_call x1, Pallas kernels, on_device(): pl.pallas_call(body, out_shape=jax.ShapeDtypeStruct(rhs.shape, F32), in_s...  69.4 us

profile of v3, /device:TPU:8, one launch (start us, length us, event | category | flops | bytes accessed | tf_op | source)
XLA Modules:
  0.0 70.7 jit_solution(2140949527136385161)
XLA Ops:
  0.0 69.4 %vcycle.1 = f32[1,1,8,4,128]{4,3,2,1,0:T(4,128)} custom-call(s32[1,1,8,14]{3,2,1,0:T(8,128)} %refs_0_.1, s32[1,1,4,4]{3,2,1,0:T(4,128)} %refs_1_.1, s32[1,1,8]{2,1,0:T(1,128)} %refs_2_.1, s32[1,1,2,14]{3,2,1,0:T(2,128)} %refs_3_.1, s32[1,1,2,4]{3,2,1,0:T(2,128)} %bitcast.1, s32[1,1,2]{2,1,0:T(1,128)} %refs_5_.1, f32[1,1,8,4,128]{4,3,2,1,0:T(4,128)} %refs_6_.1, ...), custom_call_target="tpu_custom_call" | custom-call | tf_op jit(solution)/shard_map/vcycle/pallas_call | solution.py:474
  69.4 1.3 %copy.16 = f32[1,1,8,4,128]{4,3,2,1,0:T(4,128)} copy(f32[1,1,8,4,128]{4,3,2,1,0:T(4,128)} %vcycle.1) | data formatting | bytes 32768

commit v4 on v3

--- a/solution.py
+++ b/solution.py
@@ -56,7 +56,7 @@
     w0, p0, w1, p1, sel, pp1, gp1, ps1, gsel,
     ext0, ext1, x0, r0, x1, b1, pack0, ghost0, pack1, ghost1,
     osend, oz, oy, ot, dsend, dz, dy, xsend, xg, crhs, ez, ef,
-    lsem, gs, gr, ozs, ozr, oys, oyr, dzs, dzr, dys, dyr, xs, xr, ezs, ezr, efs, efr, cs, cr,
+    heard, lsem, gs, gr, ozs, ozr, oys, oyr, dzs, dzr, dys, dyr, xs, xr, ezs, ezr, efs, efr, cs, cr,
     unroll,
 ):
     x, c, y, z = (lax.axis_index(a) for a in ("x", "c", "y", "z"))
@@ -98,7 +98,10 @@
         return (lax.rem(x + k // 4, NX), c, lax.rem(y + k % 4, NY), z)
 
     barrier = pltpu.get_barrier_semaphore()
-    peers = near + [zc_peer(k) for k in range(1, 16)] + [xy_peer(k) for k in range(1, 16)]
+    sides = [
+        (x, c, y, lax.rem(z + 1, NZ)), (x, c, y, lax.rem(z + NZ - 1, NZ)), y_peer(1), y_peer(3), x_peer(1), x_peer(3),
+    ]
+    peers = near + sides + [(x, 1 - c, y, z)]
     for peer in peers:
         pl.semaphore_signal(barrier, inc=1, device_id=peer, device_id_type=MESH)
 
@@ -141,6 +144,13 @@
     def take_near(*key):
         d, copy = due.pop(key)
         pl.when(valid[d])(copy.wait_recv)
+
+    def tell(n):
+        for side in sides:
+            pl.semaphore_signal(heard.at[n], inc=1, device_id=side, device_id_type=MESH)
+
+    def hear(n):
+        pl.semaphore_wait(heard.at[n], len(sides))
 
 
     def start_exchange(e, value, pick, pack, ghost, width, base):
@@ -241,9 +251,7 @@
     osend[0:2, :] = jnp.where(lanes == agg1[0, 0, 0], 1.0, 0.0)
     osend[2:4, :] = jnp.where(lanes == agg1[0, 0, 1], 1.0, 0.0)
     oz[me_zc] = osend[...]
-    for k in (8, 7, 9, 6, 10, 5, 11, 4, 12, 3, 13, 2, 14, 1, 15):
-        t = lax.rem(me_zc + k, 16)
-        post(("oz", k), osend, oz.at[me_zc], ozs.at[k], ozr.at[me_zc], zc_peer(k), oz.at[t], ozr.at[t])
+    tell(0)
 
     eye = jnp.where(
         lax.broadcasted_iota(jnp.int32, (256, 256), 0) == lax.broadcasted_iota(jnp.int32, (256, 256), 1), 1.0, 0.0
@@ -259,6 +267,8 @@
     for b in range(NB):
         loads.pop(b)
 
+    hear(0)
+    tell(1)
     level0_end(0)
     sweep(f0, d0, x0, ext0, cols0, w0, NB)
     level0(1)
@@ -271,14 +281,12 @@
         p0[b * BS:(b + 1) * BS, BS:2 * BS] = lo
     loads.pop(NB + 3).wait()
     post(("cin",), cin.at[c], cin.at[c], cs, cr, (x, 1 - c, y, z), cin.at[1 - c], cr)
-    for k in range(1, 16):
-        take("oz", k)
-    oy[y] = oz[...]
-    for k in (2, 1, 3):
-        t = lax.rem(y + k, NY)
-        post(("oy", k), oz, oy.at[y], oys.at[k], oyr.at[y], y_peer(k), oy.at[t], oyr.at[t])
+    hear(1)
+    tell(2)
 
     end_exchange(1, ghost0, ext0, G0, 0, NB)
+    hear(2)
+    tell(3)
     residual(f0, d0, x0, ext0, cols0, w0, NB, r0)
     parts = [[], []]
     for b in range(NB):
@@ -291,6 +299,10 @@
         b1[level] = fold(low[level * 8:level * 8 + 8])
         x1[level] = OMEGA * b1[level] / d1[level]
     level1(0)
+    hear(3)
+    for k in (8, 7, 9, 6, 10, 5, 11, 4, 12, 3, 13, 2, 14, 1, 15):
+        t = lax.rem(me_zc + k, 16)
+        post(("oz", k), osend, oz.at[me_zc], ozs.at[k], ozr.at[me_zc], zc_peer(k), oz.at[t], ozr.at[t])
 
     loads.pop(NB + 1).wait()
     for b in range(NB1):
@@ -315,13 +327,12 @@
     level1(1)
     own_part(x1, ext1, NB1)
 
-    for k in range(1, 4):
-        take("oy", k)
-    rows = []
-    for q in range(NY):
-        for t in range(8):
-            rows.append(jnp.concatenate([oy[q, 2 * t], oy[q, 2 * t + 1]], axis=0))
-    ot[...] = jnp.concatenate(rows, axis=0).T.astype(BF16)
+    for k in range(1, 16):
+        take("oz", k)
+    oy[y] = oz[...]
+    for k in (2, 1, 3):
+        t = lax.rem(y + k, NY)
+        post(("oy", k), oz, oy.at[y], oys.at[k], oyr.at[y], y_peer(k), oy.at[t], oyr.at[t])
 
     end_exchange(1, ghost1, ext1, G1, 4, NB1)
     for b in range(NB1):
@@ -334,6 +345,13 @@
         peer = zc_peer(k)
         t = lax.rem(me_zc + k, 16)
         post(("dz", k), dsend.at[peer[1]], dz.at[me_zc], dzs.at[k], dzr.at[me_zc], peer, dz.at[t], dzr.at[t])
+    for k in range(1, 4):
+        take("oy", k)
+    rows = []
+    for q in range(NY):
+        for t in range(8):
+            rows.append(jnp.concatenate([oy[q, 2 * t], oy[q, 2 * t + 1]], axis=0))
+    ot[...] = jnp.concatenate(rows, axis=0).T.astype(BF16)
     take("cin")
     for k in range(1, 16):
         take("dz", k)
@@ -461,7 +479,7 @@
         V((2, 4, BS), F32), V((16, 4, BS), F32), V((4, 16, 4, BS), F32),
         V((64, 256), F32), V((4, 64, 256), F32), V((2, 64, BS), F32),
         V((16, 4, BS), F32), V((16, 4, 4, BS), F32),
-        dma((NB + 13,)), dma((10, 4)), dma((10, 4)),
+        pltpu.SemaphoreType.REGULAR((4,)), dma((NB + 13,)), dma((10, 4)), dma((10, 4)),
         dma((16,)), dma((16,)), dma((4,)), dma((4,)),
         dma((16,)), dma((16,)), dma((4,)), dma((4,)),
         dma((4,)), dma((4,)), dma((16,)), dma((16,)), dma((16,)), dma((16,)),

time: 70.9 us -> 68.5 us (0.966)
  Pallas kernels: 69.4 us -> 67 us
    pallas_call x1, Pallas kernels: 69.4 us -> 67 us  [on_device(): pl.pallas_call(body, out_shape=jax.ShapeDtypeStruct(rhs.shape, F32), in_s...]
where the time goes in v4:
time: 68.5 us; the launch traced here: 68.3 us
  Pallas kernels  67 us (98%)
  local copies, waits for them, and re-layouts  1.32 us (2%)
    pallas_call x1, Pallas kernels, on_device(): pl.pallas_call(body, out_shape=jax.ShapeDtypeStruct(rhs.shape, F32), in_s...  67 us

profile of v4, /device:TPU:8, one launch (start us, length us, event | category | flops | bytes accessed | tf_op | source)
XLA Modules:
  0.0 68.3 jit_solution(18356044606841534857)
XLA Ops:
  0.0 67.0 %vcycle.1 = f32[1,1,8,4,128]{4,3,2,1,0:T(4,128)} custom-call(s32[1,1,8,14]{3,2,1,0:T(8,128)} %refs_0_.1, s32[1,1,4,4]{3,2,1,0:T(4,128)} %refs_1_.1, s32[1,1,8]{2,1,0:T(1,128)} %refs_2_.1, s32[1,1,2,14]{3,2,1,0:T(2,128)} %refs_3_.1, s32[1,1,2,4]{3,2,1,0:T(2,128)} %bitcast.1, s32[1,1,2]{2,1,0:T(1,128)} %refs_5_.1, f32[1,1,8,4,128]{4,3,2,1,0:T(4,128)} %refs_6_.1, ...), custom_call_target="tpu_custom_call" | custom-call | tf_op jit(solution)/shard_map/vcycle/pallas_call | solution.py:492
  67.0 1.3 %copy.16 = f32[1,1,8,4,128]{4,3,2,1,0:T(4,128)} copy(f32[1,1,8,4,128]{4,3,2,1,0:T(4,128)} %vcycle.1) | data formatting | bytes 32768

commit v5 on v4

--- a/solution.py
+++ b/solution.py
@@ -101,9 +101,15 @@
     sides = [
         (x, c, y, lax.rem(z + 1, NZ)), (x, c, y, lax.rem(z + NZ - 1, NZ)), y_peer(1), y_peer(3), x_peer(1), x_peer(3),
     ]
-    peers = near + sides + [(x, 1 - c, y, z)]
+    peers = sides + [(x, 1 - c, y, z)]
     for peer in peers:
         pl.semaphore_signal(barrier, inc=1, device_id=peer, device_id_type=MESH)
+
+    def greet(d):
+        pl.semaphore_signal(barrier, inc=1, device_id=near[d], device_id_type=MESH)
+
+    for d in range(4):
+        pl.when(reaches[d])(lambda d=d: greet(d))
 
     for i, (src, dst) in enumerate(
         ((sends0_h, sends0), (sends1_h, sends1), (agg1_h, agg1), (cols0_h, cols0), (agg0_h, agg0), (cols1_h, cols1))
@@ -154,10 +160,9 @@
 
 
     def start_exchange(e, value, pick, pack, ghost, width, base):
-        for d in range(4):
+        for d in (2, 3, 0, 1):
             for g in range(width):
                 pack[e, d, g] = value[pick(d, g)]
-        for d in range(4):
             post_near((base + e, d), pack.at[e, d], ghost.at[e, d], gs.at[base + e, d], gr.at[base + e, d], d)
 
     def own_part(value, ext, count):
@@ -228,7 +233,7 @@
         loads.pop(NB + n).wait()
     for b in range(NB):
         x0[b] = OMEGA * f0[b] / d0[b]
-    pl.semaphore_wait(barrier, len(peers))
+    pl.semaphore_wait(barrier, len(peers) + sum(jnp.where(v, 1, 0) for v in valid))
     level0(0)
 
     loads.pop(NB + 2).wait()
@@ -395,7 +400,7 @@
                     acc[(g * 2 + r) * 4 + m] = acc[(g * 2 + r) * 4 + m] + a * vec[r]
         return tuple(acc)
 
-    acc = lax.fori_loop(0, 64, mat, tuple(jnp.zeros((8, BS), F32) for _ in range(16)), unroll=4)
+    acc = lax.fori_loop(0, 64, mat, tuple(jnp.zeros((8, BS), F32) for _ in range(16)), unroll=16)
     zl = lax.rem(z, 4)
     chunks = []
     for q in range(4):

time: 68.5 us -> 68.2 us (level)
  no operation moved by 1% of the time
where the time goes in v5:
time: 68.2 us; the launch traced here: 68 us
  Pallas kernels  66.6 us (98%)
  local copies, waits for them, and re-layouts  1.32 us (2%)
    pallas_call x1, Pallas kernels, on_device(): pl.pallas_call(body, out_shape=jax.ShapeDtypeStruct(rhs.shape, F32), in_s...  66.6 us

profile of v5, /device:TPU:8, one launch (start us, length us, event | category | flops | bytes accessed | tf_op | source)
XLA Modules:
  0.0 68.0 jit_solution(3502058394754216337)
XLA Ops:
  0.0 66.6 %vcycle.1 = f32[1,1,8,4,128]{4,3,2,1,0:T(4,128)} custom-call(s32[1,1,8,14]{3,2,1,0:T(8,128)} %refs_0_.1, s32[1,1,4,4]{3,2,1,0:T(4,128)} %refs_1_.1, s32[1,1,8]{2,1,0:T(1,128)} %refs_2_.1, s32[1,1,2,14]{3,2,1,0:T(2,128)} %refs_3_.1, s32[1,1,2,4]{3,2,1,0:T(2,128)} %bitcast.1, s32[1,1,2]{2,1,0:T(1,128)} %refs_5_.1, f32[1,1,8,4,128]{4,3,2,1,0:T(4,128)} %refs_6_.1, ...), custom_call_target="tpu_custom_call" | custom-call | tf_op jit(solution)/shard_map/vcycle/pallas_call | solution.py:497
  66.6 1.3 %copy.16 = f32[1,1,8,4,128]{4,3,2,1,0:T(4,128)} copy(f32[1,1,8,4,128]{4,3,2,1,0:T(4,128)} %vcycle.1) | data formatting | bytes 32768
